TPU v7x, 256 devices: a whole 4x4x8 slice. The times are simulated.
256 devices in a mesh: row: 8 (over z), col: 8 (over x_lo, y), layer: 4 (over x_hi, core).
Axes of the slice: x: 4 (x_hi: 2, x_lo: 2; x = x_hi * 2 + x_lo), y: 4, z: 8, core: 2. Of those that a mesh axis runs over, the one named last changes fastest.
Arguments:
- tokens: bfloat16 [5120, 6144], P('row', 'layer'), may hold values from -6 to 6
- expert_ids: int32 [5120, 2], replicated, may hold values from 0 to 7, all different within a row; in each aligned block of 5120 rows (0 to 5119, 5120 to 10239, ...) at most 2560 rows name the same one
- w_gate: bfloat16 [2, 6144, 8192], P(None, 'layer', ('row', 'col')), may hold values from -0.078125 to 0.078125
- w_up: bfloat16 [2, 6144, 8192], P(None, 'layer', ('row', 'col')), may hold values from -0.078125 to 0.078125
Outputs:
- hidden: bfloat16 [2, 2560, 8192], P(None, ('col', 'layer'), 'row')
Inputs may be any that keep to these rules, and one draw needn't show every extreme that they name: `expert_ids`: each token names 2 different experts. No expert is named by more than 2560 tokens, a bound that some block reaches.
All inputs are finite; a program needn't handle non-finite values.
Results may differ from a plain program's by a relative error of at most 0.0012.
Values may be sent and summed in bfloat16 or wider, within the bound.
No kernel may reach another device: no remote copies, remote signals or barrier semaphores. Data moves between devices by JAX's collectives and lax.ppermute only.
A program may use at most 128 MiB of HBM per device.

v0:
```python
import jax
import jax.numpy as jnp
from jax import lax
from jax.sharding import PartitionSpec as P

SLOTS_DEV = 80


def laid_out(tiles, dim):
    tiles = jnp.moveaxis(tiles, 0, dim)
    shape = tiles.shape
    return tiles.reshape(*shape[:dim], shape[dim] * shape[dim + 1], *shape[dim + 2 :])


def on_gathered_pieces(x, axis, dim, apply, out_dim):
    size, span = (lax.axis_size(axis), x.shape[dim])
    count = 2 if span % 2 == 0 else 1
    done, length = ([], span // count)
    for k in range(count):
        piece = lax.slice_in_dim(x, k * length, (k + 1) * length, axis=dim)
        starts = jnp.arange(size) * span + k * length
        done.append(jax.vmap(apply)(lax.all_gather(piece, axis), starts))
    return laid_out(jnp.concatenate(done, axis=out_dim + 1), out_dim)


def shards(tokens, expert_ids, w_gate, w_up):
    col_count = lax.axis_size("col")
    layer_count = lax.axis_size("layer")
    row_count = lax.axis_size("row")
    col_index = lax.axis_index("col")
    row_index = lax.axis_index("row")
    experts = w_gate.shape[0]
    capacity = SLOTS_DEV * col_count * layer_count
    slot_block = capacity // col_count
    local_rows = tokens.shape[0]
    tok_count = local_rows * row_count
    expert_range = jnp.arange(experts, dtype=jnp.int32)
    member = jnp.any(expert_ids[:, :, None] == expert_range[None, None, :], axis=1).astype(
        jnp.int32
    )
    slot_rank = jnp.cumsum(member, axis=0) - member
    target = jnp.where(member > 0, slot_rank, capacity)
    token_range = jnp.broadcast_to(jnp.arange(tok_count, dtype=jnp.int32)[:, None], target.shape)
    slot_table = (
        jnp.zeros((experts, capacity + 1), jnp.int32)
        .at[expert_range[None, :], target]
        .set(token_range)
    )
    counts = jnp.sum(member, axis=0)
    slot_start = col_index * slot_block
    picked = lax.dynamic_slice_in_dim(slot_table, slot_start, slot_block, 1)
    position = slot_start + jnp.arange(slot_block, dtype=jnp.int32)
    live_mask = position[None, :] < counts[:, None]
    row_start = row_index * local_rows
    local_pick = picked - row_start
    inside = live_mask & (local_pick >= 0) & (local_pick < local_rows)
    own_rows = tokens[jnp.clip(local_pick, 0, local_rows - 1)]
    placed = jnp.where(inside[:, :, None], own_rows, jnp.zeros((), tokens.dtype)).astype(
        jnp.float32
    )
    slot_rows = lax.psum(placed.astype(jnp.bfloat16), "row")
    stacked = jnp.stack((w_gate, w_up))

    def project(piece, start):
        return jnp.einsum("ecd,pedf->pecf", slot_rows, piece, preferred_element_type=jnp.float32)

    totals = on_gathered_pieces(stacked, "col", 3, project, 3)
    parts = lax.psum_scatter(totals, "layer", scatter_dimension=2, tiled=True)
    return (jax.nn.silu(parts[0]) * parts[1]).astype(jnp.bfloat16)


def solution(mesh):
    in_specs = (
        P("row", "layer"),
        P(),
        P(None, "layer", ("row", "col")),
        P(None, "layer", ("row", "col")),
    )
    out_specs = P(None, ("col", "layer"), "row")
    return jax.shard_map(shards, mesh=mesh, in_specs=in_specs, out_specs=out_specs, check_vma=False)
```

profile of v0, /device:TPU:1, one launch (start us, length us, event | category | flops | bytes accessed | tf_op | source)
XLA Modules:
  0.0 269.2 jit_solution(11576271825753675574)
XLA Ops:
  7.4 1.5 copy.19
  8.9 1.4 copy.20
  10.4 1.3 fusion.10
  11.8 0.7 all-gather.7.cloned.1.call-update
  12.5 0.9 compare_reduce_fusion
  13.4 0.6 reduce-window.6
  14.0 0.2 slice_reduce_fusion
  14.2 0.2 reduce-window.9
  14.5 0.2 convert_reduce_fusion
  14.7 0.1 multiply_reduce_fusion
  14.8 0.1 and_reduce_fusion
  15.0 2.3 copy.22
  17.3 3.1 %reshape.40 = s32[10240]{0:T(1024)S(1)} reshape(s32[5120,2]{1,0:T(8,128)} %copy.22) | data formatting | bytes 81920
  20.4 1.7 broadcast_in_dim.46
  22.1 3.1 %reshape.42 = s32[10240]{0:T(1024)S(1)} reshape(s32[5120,2]{1,0:T(8,128)} %broadcast_in_dim.46) | data formatting | bytes 81920 | tf_op jit(solution)/shard_map/broadcast_in_dim | solution.py:43
  25.2 38.0 %scatter_custom_fusion = s32[5122]{0:T(1024)S(1)} fusion(s32[10240]{0:T(1024)S(1)} %reshape.40, s32[10240]{0:T(1024)S(1)} %reshape.42, s32[]{:T(128)} %constant.16.clone.1), kind=kCustom, calls=%fused_computation.33 | custom fusion | bytes 20492
  63.1 0.1 reshape.30
  63.2 0.1 compare_select_fusion.2
  63.4 3.7 %gather_fusion = bf16[640,1536]{1,0:T(8,128)(2,1)} fusion(bf16[640,1536]{1,0:T(8,128)(2,1)S(1)} %copy-done, s32[1024]{0:T(1024)S(1)} %pad_clamp_fusion), kind=kCustom, calls=%fused_computation | custom fusion | bytes 3934720 | tf_op jit(solution)/shard_map/gather | solution.py:57
  67.2 3.1 %broadcast_select_fusion = bf16[2,320,1536]{2,1,0:T(8,128)(2,1)} fusion(bf16[2,320,1536]{2,1,0:T(8,128)(2,1)} %bitcast.59, pred[2,320]{1,0:T(4,128)(4,1)S(1)} %compare_and_fusion), kind=kLoop, calls=%fused_computation.7 | loop fusion | flops 983040 | bytes 3932800 | tf_op jit(solution)/shard_map/jit(_where)/select_n | solution.py:58
  70.3 0.2 reduce-scatter.2.cloned.1.call-start
  70.5 19.7 %all-gather.5.cloned.1.call-done = bf16[16,2,1536,64]{2,3,1,0:T(8,128)(2,1)} async-done(((bf16[2,2,1536,64]{2,3,1,0:T(8,128)(2,1)}), bf16[16,2,1536,64]{2,3,1,0:T(8,128)(2,1)}) %all-gather.5.cloned.1.call-update) | async-done | bytes 6291472 | tf_op jit(solution)/shard_map/all_gather | solution.py:22
  90.2 6.1 %copy.21 = bf16[16,2,1536,64]{2,3,0,1:T(8,128)(2,1)} copy(bf16[16,2,1536,64]{2,3,1,0:T(8,128)(2,1)} %all-gather.5.cloned.1.call-done) | data formatting | bytes 12582912 | tf_op jit(solution)/shard_map/all_gather | solution.py:22
  96.4 69.2 %all-gather.7.cloned.1.call-done = bf16[16,2,1536,64]{2,3,1,0:T(8,128)(2,1)} async-done(((bf16[2,2,1536,64]{2,3,1,0:T(8,128)(2,1)}), bf16[16,2,1536,64]{2,3,1,0:T(8,128)(2,1)}) %all-gather.7.cloned.1.call-update) | async-done | bytes 6291472 | tf_op jit(solution)/shard_map/all_gather | solution.py:22
  165.6 6.1 %copy.23 = bf16[16,2,1536,64]{2,3,0,1:T(8,128)(2,1)} copy(bf16[16,2,1536,64]{2,3,1,0:T(8,128)(2,1)} %all-gather.7.cloned.1.call-done) | data formatting | bytes 12582912 | tf_op jit(solution)/shard_map/all_gather | solution.py:22
  171.7 6.3 %fusion.4 = f32[8,2,2,320,64]{3,4,1,0,2:T(8,128)S(1)} fusion(bf16[8,2,2,1536,64]{3,4,1,0,2:T(8,128)(2,1)} %bitcast.60, bf16[2,320,1536]{2,1,0:T(8,128)(2,1)} %all-reduce.2.cloned.1.call-done), kind=kOutput, calls=%fused_computation.8 | convolution fusion | flops 2013265920 | bytes 10878976 | tf_op jit(solution)/shard_map/vmap(ecd,pedf->pecf)/dot_general | solution.py:65
  178.0 3.4 %fusion.7 = f32[8,2,2,320,64]{3,4,1,0,2:T(8,128)S(1)} fusion(bf16[8,2,2,1536,64]{3,4,1,0,2:T(8,128)(2,1)S(1)} %bitcast.61, bf16[2,320,1536]{2,1,0:T(8,128)(2,1)S(1)} %copy-done.5), kind=kOutput, calls=%fused_computation.9 | convolution fusion | flops 2013265920 | bytes 10878976 | tf_op jit(solution)/shard_map/vmap(ecd,pedf->pecf)/dot_general | solution.py:65
  181.4 3.1 %maximum_bitcast_fusion = f32[2,2,320,8,128]{2,4,0,3,1:T(8,128)} fusion(f32[8,2,2,320,64]{3,4,1,0,2:T(8,128)S(1)} %fusion.7, f32[8,2,2,320,64]{3,4,1,0,2:T(8,128)S(1)} %fusion.4), kind=kLoop, calls=%fused_computation.2 | loop fusion | flops 1310720 | bytes 10485760 | tf_op jit(solution)/shard_map/transpose | solution.py:10
  184.5 6.3 %copy.24 = f32[2,2,320,8,128]{4,3,2,1,0:T(8,128)} copy(f32[2,2,320,8,128]{2,4,0,3,1:T(8,128)} %maximum_bitcast_fusion) | data formatting | bytes 10485760 | tf_op jit(solution)/shard_map/transpose | solution.py:10
  190.8 6.7 %reshape.26 = f32[2,2,320,1024]{3,2,1,0:T(8,128)} reshape(f32[2,2,320,8,128]{4,3,2,1,0:T(8,128)} %copy.24) | data formatting | bytes 10485760 | tf_op jit(solution)/shard_map/reshape | solution.py:12
  197.6 62.0 %reduce-scatter.2.cloned.1.call-done = f32[2,2,80,1024]{3,2,1,0:T(8,128)} async-done(((f32[2,2,320,1024]{3,2,1,0:T(8,128)}), f32[2,2,80,1024]{3,2,1,0:T(8,128)}) %reduce-scatter.2.cloned.1.call-update) | async-done | bytes 1310736 | tf_op jit(solution)/shard_map/reduce_scatter | solution.py:68
  259.6 2.2 fusion.12
  (28 shorter events, 0.5 us)
Async XLA Ops:
  7.4 56.0 %copy-start = (bf16[640,1536]{1,0:T(8,128)(2,1)S(1)}, bf16[640,1536]{1,0:T(8,128)(2,1)}, u32[]{:S(2)}) copy-start(bf16[640,1536]{1,0:T(8,128)(2,1)} %param.4) | copy-start | bytes 5898244
  7.4 82.9 %all-gather.5.cloned.1.call-start = ((), (), s32[]{:S(2)}) async-start(), calls=%async_computation.3 | async-start | bytes 7077888 | tf_op jit(solution)/shard_map/all_gather | solution.py:22
  10.3 4.4 %copy-start.4 = (s32[2]{0:T(128)S(1)}, s32[2]{0:T(128)}, u32[]{:S(2)}) copy-start(s32[2]{0:T(128)} %constant.40) | copy-start | bytes 28
  10.3 4.5 %copy-start.3 = (s32[2]{0:T(128)S(1)}, s32[2]{0:T(128)}, u32[]{:S(2)}) copy-start(s32[2]{0:T(128)} %constant.43) | copy-start | bytes 28
  11.7 153.9 %all-gather.7.cloned.1.call-start = ((), (), s32[]{:S(2)}) async-start(), calls=%async_computation.4 | async-start | bytes 7077888 | tf_op jit(solution)/shard_map/all_gather | solution.py:22
  12.5 159.2 %all-reduce.2.cloned.1.call-start = ((), (), s32[]{:S(2)}) async-start(), calls=%async_computation.1 | async-start | bytes 3932160 | tf_op jit(solution)/shard_map/psum | solution.py:61
  70.3 189.3 %reduce-scatter.2.cloned.1.call-start = ((), (), s32[]{:S(2)}) async-start(), calls=%async_computation.2 | async-start | bytes 6553600 | tf_op jit(solution)/shard_map/reduce_scatter | solution.py:68
  171.7 6.3 %copy-start.2 = (bf16[16,2,1536,64]{2,3,0,1:T(8,128)(2,1)S(1)}, bf16[16,2,1536,64]{2,3,0,1:T(8,128)(2,1)}, u32[]{:S(2)}) copy-start(bf16[16,2,1536,64]{2,3,0,1:T(8,128)(2,1)} %copy.23) | copy-start | bytes 18874372
  171.7 6.3 %copy-start.5 = (bf16[2,320,1536]{2,1,0:T(8,128)(2,1)S(1)}, bf16[2,320,1536]{2,1,0:T(8,128)(2,1)}, u32[]{:S(2)}) copy-start(bf16[2,320,1536]{2,1,0:T(8,128)(2,1)} %all-reduce.2.cloned.1.call-done) | copy-start | bytes 5898244
  197.5 64.2 %copy-start.1 = (bf16[640,1536]{1,0:T(8,128)(2,1)S(1)}, bf16[640,1536]{1,0:T(8,128)(2,1)}, u32[]{:S(2)}) copy-start(bf16[640,1536]{1,0:T(8,128)(2,1)} %param.4) | copy-start | bytes 5898244
Sparse Core Ops, SparseCore 0:
  11.8 78.3 all-gather.4
  92.0 73.5 all-gather.6
Sparse Core Ops, SparseCore 1:
  70.4 81.0 all-reduce.1
  197.6 61.9 reduce-scatter.1
where the time goes:
time: 270 us; the launch traced here: 269 us
  waiting for transfers between devices  152 us (56%)
  local copies, waits for them, and re-layouts  80.4 us (30%)
  between operations  15 us (6%)
  other arithmetic  12.1 us (4%)
  matrix products  9.66 us (4%)
    all_gather x2, waiting for transfers between devices, on_gathered_pieces(): done.append(jax.vmap(apply)(lax.all_gather(piece, axis), starts))  88.9 us
    reduce_scatter x1, waiting for transfers between devices, shards(): parts = lax.psum_scatter(totals, 'layer', scatter_dimension=2, tiled=True)  62 us
    unnamed x18, local copies, waits for them, and re-layouts  46.3 us
    all_gather x2, local copies, waits for them, and re-layouts, on_gathered_pieces(): done.append(jax.vmap(apply)(lax.all_gather(piece, axis), starts))  12.2 us
    dot_general x2, matrix products, project(): jnp.einsum('ecd,pedf->pecf', slot_rows, piece, preferred_element_type=jnp...  9.66 us
    reshape x1, local copies, waits for them, and re-layouts, laid_out(): tiles.reshape(*shape[:dim], shape[dim] * shape[dim + 1], *shape[dim + 2:])  6.73 us
    transpose x1, local copies, waits for them, and re-layouts, laid_out(): tiles = jnp.moveaxis(tiles, 0, dim)  6.3 us
  transfers between devices with their start and end apart: 4, of which 3 were waited for; matrix products, arithmetic and copies ran while one was open for 26% of the time, Pallas kernels for 0%

commit v1 on v0

v1 whole, which is shorter than its diff:
```python
import jax
import jax.numpy as jnp
from jax import lax
from jax.experimental import pallas as pl
from jax.experimental.pallas import tpu as pltpu
from jax.sharding import PartitionSpec as P


ROWS = 8
SETS = 4
HALVES = 2
QUARTERS = 4
SLOTS_DEV = 80
SEND = 168
DEAL = 21
GROUP = HALVES * SETS * DEAL
DEAL_PAD = 24
STEPS = 256
TOP = 32767.0


def y_perm(step):
    return [(y, (y + step) % SETS) for y in range(SETS)]


def y_cross_perm(step):
    return [(2 * y + k, 2 * ((y + step) % SETS) + 1 - k) for y in range(SETS) for k in range(2)]


def z_perm(step):
    return [(z, (z + step) % ROWS) for z in range(ROWS)]


SWAP = [(0, 1), (1, 0)]


def below(n, s):
    return (n + (SETS - 1) - s) >> 2


def pick_of(pair, index):
    return lax.dynamic_index_in_dim(pair, index, 0, keepdims=False)


def weights_of_ring(w_gate, w_up, core):
    near = jnp.stack([pick_of(w_gate, core), pick_of(w_up, core)])
    far = jnp.stack([pick_of(w_gate, 1 - core), pick_of(w_up, 1 - core)])
    near1 = lax.ppermute(near, "y", y_perm(1))
    far2 = lax.ppermute(far, ("y", "core"), y_cross_perm(-1))
    far1 = lax.ppermute(far, ("y", "core"), y_cross_perm(1))
    near2 = lax.ppermute(near, "y", y_perm(-1))
    far0 = lax.ppermute(far, "core", SWAP)
    near3 = lax.ppermute(near1, "y", y_perm(1))
    far3 = lax.ppermute(far2, "y", y_perm(-1))
    return [near, near1, near2, near3], [far0, far1, far2, far3]


def rows_of_ring(chunk):
    got, up, down = [chunk], chunk, chunk
    for _ in range(1, 4):
        up = lax.ppermute(up, "z", z_perm(1))
        down = lax.ppermute(down, "z", z_perm(-1))
        got += [up, down]
    cut = 88
    first = lax.ppermute(up[:cut], "z", z_perm(1))
    second = lax.ppermute(down[cut:], "z", z_perm(-1))
    return got + [jnp.concatenate([first, second])]


LANES = 128
VMEM = pl.BlockSpec(memory_space=pltpu.VMEM)
SMEM = pl.BlockSpec(memory_space=pltpu.SMEM)


def iota(shape, dim):
    return lax.broadcasted_iota(jnp.int32, shape, dim)


def exact_dot(a, b):
    return jnp.dot(a.astype(jnp.bfloat16), b.astype(jnp.bfloat16), preferred_element_type=jnp.float32)


def rows_product(a, b):
    return lax.dot_general(a, b, (((1,), (1,)), ((), ())), preferred_element_type=jnp.float32)


def one_hot(values, count):
    wide = [
        (iota((count, LANES), 0) == values[i : i + 1]).astype(jnp.float32).astype(jnp.bfloat16)
        for i in range(values.shape[0])
    ]
    return jnp.concatenate(wide, axis=1)


def deal_kernel(here, code, tokens, chunk, rank, own, at):
    blocks = code.shape[0]
    per = blocks // ROWS
    kinds = [(code[...] == k).astype(jnp.float32) for k in (1, 3, 2)]
    before = (iota((LANES, LANES), 0) < iota((LANES, LANES), 1)).astype(jnp.float32)
    ones = jnp.ones((LANES, LANES), jnp.float32)
    r, c = iota((blocks, blocks), 0), iota((blocks, blocks), 1)
    earlier = (c < r).astype(jnp.float32)
    planes = (c < r // per * per).astype(jnp.float32)
    ranks, firsts = [], []
    for kind in kinds:
        sums = exact_dot(kind, ones)
        ranks.append((exact_dot(kind, before) + exact_dot(earlier, sums)).astype(jnp.int32))
        firsts.append(exact_dot(planes, sums).astype(jnp.int32))
    which = jnp.where(code[...] == 3, ranks[1], jnp.where(code[...] == 2, ranks[2], ranks[0]))
    mod = jnp.where(code[...] > 0, which & (SETS - 1), -1)
    place = sum(below(n, mod) - below(f, mod) for n, f in zip(ranks, firsts))
    place = jnp.where(mod == here[1], place, -1)
    own[...] = mod
    for k in range(3):
        rank[k] = ranks[k]
    for q in range(ROWS):
        at[q, :per] = place[q * per : (q + 1) * per]
    send = one_hot(at[here[0]][:per], SEND)
    chunk[...] = jnp.dot(send, tokens[...], preferred_element_type=jnp.float32).astype(jnp.bfloat16)


def lists_kernel(here, code, rank, own, at, lists, places):
    z, y, low, group_here, core = (here[i] for i in range(5))
    per = code.shape[0] // ROWS
    n_blocks = HALVES * SETS * QUARTERS
    mine = own[...] == y
    targets, slot_at, from_at = [], [], []
    for e in range(2):
        member = (code[...] == 1 + e) | (code[...] == 3)
        slot = rank[e] + rank[e + 1]
        seen = below(rank[e], y) + below(rank[e + 1], y)
        in_set = mine & member
        base = jnp.zeros_like(slot)
        for b in range(1, n_blocks):
            count = jnp.sum((in_set & (slot < b * SLOTS_DEV)).astype(jnp.int32))
            base = jnp.where(slot >= b * SLOTS_DEV, count, base)
        b = (slot * 52429) >> 22
        group = (b & (QUARTERS - 1)) ^ group_here
        target = group * GROUP + (b >> 2) * DEAL + seen - base
        targets.append(jnp.where(in_set, target + 1, 0))
        inside = member & (slot >= low) & (slot < low + SLOTS_DEV)
        early = member & (slot < low)
        nth = own[...] * DEAL_PAD
        for k, kind in ((e, 1 if e == 0 else 3), (e + 1, 3 if e == 0 else 2)):
            first = jnp.sum((early & (code[...] == kind)).astype(jnp.int32))
            nth += below(rank[k], own[...]) - below(first, own[...])
        slot_at.append(jnp.where(inside, slot - low, -1))
        from_at.append(jnp.where(inside, nth, -1))
    own_expert = jnp.where(core == 0, targets[0], targets[1])
    other = jnp.where(core == 0, targets[1], targets[0])
    turned = jnp.where((other - 1) // GROUP % 2 == 0, other + GROUP, other - GROUP)
    other = jnp.where(other > 0, turned, 0)
    parts = [own_expert >> 5, own_expert & 31, other >> 5, other & 31]
    parts = [p.astype(jnp.float32).astype(jnp.bfloat16) for p in parts]
    for q in range(ROWS):
        distance = (q - z + ROWS) & (ROWS - 1)
        turn = jnp.where(distance <= ROWS // 2, 2 * distance, 2 * (ROWS - distance) - 1)
        turn = jnp.where(distance == ROWS // 2, ROWS - 1, turn)
        span = slice(q * per, (q + 1) * per)
        values = [jnp.concatenate([p[i : i + 1] for i in range(q * per, (q + 1) * per)], axis=1) for p in parts]
        values = jnp.concatenate(values + values, axis=0)
        spread = one_hot(at[q][:per], SEND)
        lists[turn] = rows_product(values, spread)
    for i in range(2):
        total = jnp.zeros(places.shape[1:], jnp.float32)
        for q in range(ROWS):
            span = slice(q * per, (q + 1) * per)
            total += rows_product(
                one_hot(slot_at[i][span], SLOTS_DEV), one_hot(from_at[i][span], SETS * DEAL_PAD)
            )
        places[i] = total.astype(jnp.bfloat16)


def coded(values, out, column):
    rows = values.shape[0]
    top = jnp.maximum(jnp.max(jnp.abs(values), axis=1, keepdims=True), 1e-37)
    log = jnp.ceil(jnp.log2(top) * STEPS)
    parts = jnp.clip(values * (TOP * jnp.exp2(log * (-1.0 / STEPS))), -TOP, TOP)
    span = slice(column * LANES, (column + 1) * LANES)
    out[:rows, span] = jnp.round(parts).astype(jnp.int32).astype(jnp.int16)
    tail = jnp.zeros((out.shape[0] - rows, LANES), jnp.float32)
    for i in range(0, rows, LANES):
        some = log[i : i + LANES]
        there = iota((some.shape[0], LANES), 0) == iota((some.shape[0], LANES), 1)
        line = jnp.sum(jnp.where(there, some, 0.0), axis=0, keepdims=True)
        tail = jnp.where(iota(tail.shape, 0) == i // LANES, line, tail)
    out[rows:, span] = tail.astype(jnp.int32).astype(jnp.int16)


def decoded(code, column, rows):
    span = slice(column * LANES, (column + 1) * LANES)
    tail = code[rows:, span].astype(jnp.int32).astype(jnp.float32)
    logs = []
    for i in range(0, rows, LANES):
        count = min(LANES, rows - i)
        there = iota((count, LANES), 0) == iota((count, LANES), 1)
        line = tail[i // LANES : i // LANES + 1]
        logs.append(jnp.sum(jnp.where(there, line, 0.0), axis=1, keepdims=True))
    scale = jnp.exp2(jnp.concatenate(logs, axis=0) * (1.0 / STEPS)) * (1.0 / TOP)
    return code[:rows, span].astype(jnp.int32).astype(jnp.float32) * scale


def product_kernel(x, *refs):
    count = (len(refs) - 2) // 2
    near, far, keep, give = refs[:count], refs[count : 2 * count], refs[-2], refs[-1]
    n_half = keep.shape[0]
    for j, (a, b) in enumerate(zip(near, far)):
        w = jnp.concatenate(
            [jnp.concatenate([a[0], a[1]], axis=1), jnp.concatenate([b[0], b[1]], axis=1)], axis=0
        )
        sums = jnp.dot(x[n_half:], w, preferred_element_type=jnp.float32)
        for i in range(2):
            coded(sums[:, i * LANES : (i + 1) * LANES], give, 2 * j + i)
        sums = jnp.dot(x[:n_half], w, preferred_element_type=jnp.float32)
        keep[:, 2 * j * LANES : 2 * (j + 1) * LANES] = sums


def product(x, near, far):
    rows, depth = x.shape
    width = len(near) * 2 * near[0].shape[2]
    return pl.pallas_call(
        product_kernel,
        out_shape=(
            jax.ShapeDtypeStruct((rows // 2, width), jnp.float32),
            jax.ShapeDtypeStruct((rows // 2 + 16, width), jnp.int16),
        ),
        in_specs=[VMEM] * (1 + 2 * len(near)),
        out_specs=(VMEM,) * 2,
        compiler_params=pltpu.CompilerParams(vmem_limit_bytes=24 << 20),
        cost_estimate=pl.CostEstimate(
            flops=2 * rows * depth * width,
            bytes_accessed=4 * rows * width + 2 * depth * (rows + width),
            transcendentals=0,
        ),
    )(x, *near, *far)


def gated_kernel(here, *refs):
    keeps, codes, out = refs[:2], refs[2:4], refs[4]
    rows = keeps[0].shape[0]
    y, core = here[1], here[4]
    for o, ahead in enumerate((0, SETS - 1, 1, 2)):
        keep, code, j = keeps[o // 2], codes[o // 2], o % 2
        gate, up = (
            keep[:, (2 * j + i) * LANES : (2 * j + i + 1) * LANES] + decoded(code, 2 * j + i, rows)
            for i in range(2)
        )
        hidden = gate / (1.0 + jnp.exp(-gate)) * up
        piece = (y + ahead) & (SETS - 1)
        pad = jnp.zeros((DEAL_PAD - DEAL, LANES), jnp.float32)
        for k in range(2):
            for c in range(HALVES * SETS):
                first = k * GROUP + c * DEAL
                some = jnp.concatenate([hidden[first : first + DEAL], pad], axis=0)
                out[2 * c + (k ^ core), piece] = some.astype(jnp.bfloat16)


def placed_kernel(got, places, out):
    for e in range(2):
        for h in range(HALVES):
            lines = [
                jnp.concatenate([got[(h * SETS + s) * 2 + e, p] for p in range(SETS)], axis=1)
                for s in range(SETS)
            ]
            rows = jnp.concatenate(lines, axis=0)
            wide = rows.shape[1]
            out[e, :, h * wide : (h + 1) * wide] = jnp.dot(
                places[e], rows, preferred_element_type=jnp.float32
            ).astype(jnp.bfloat16)


def shards(tokens, expert_ids, w_gate, w_up):
    z = lax.axis_index("z")
    y = lax.axis_index("y")
    x_lo = lax.axis_index("x_lo")
    x_hi = lax.axis_index("x_hi")
    core = lax.axis_index("core")
    near, far = weights_of_ring(w_gate, w_up, core)

    blocks = expert_ids.shape[0] // LANES
    ids = expert_ids.T
    code = sum(jnp.any(ids == e, axis=0).astype(jnp.int32) * (1 + e) for e in range(2))
    code = code.reshape(blocks, LANES)
    low = ((x_lo * SETS + y) * QUARTERS + 2 * x_hi + core) * SLOTS_DEV
    here = jnp.stack([z, y, low, 2 * x_hi + core, core]).astype(jnp.int32)
    chunk, rank, own, at = pl.pallas_call(
        deal_kernel,
        out_shape=(
            jax.ShapeDtypeStruct((SEND, tokens.shape[1]), jnp.bfloat16),
            jax.ShapeDtypeStruct((3, blocks, LANES), jnp.int32),
            jax.ShapeDtypeStruct((blocks, LANES), jnp.int32),
            jax.ShapeDtypeStruct((ROWS, 8, LANES), jnp.int32),
        ),
        in_specs=[SMEM, VMEM, VMEM],
        out_specs=(VMEM,) * 4,
        compiler_params=pltpu.CompilerParams(vmem_limit_bytes=8 << 20),
        cost_estimate=pl.CostEstimate(flops=1 << 30, bytes_accessed=1 << 22, transcendentals=0),
    )(here, code, tokens)
    chunks = rows_of_ring(chunk)

    moved, places = pl.pallas_call(
        lists_kernel,
        out_shape=(
            jax.ShapeDtypeStruct((ROWS, 8, SEND), jnp.float32),
            jax.ShapeDtypeStruct((2, SLOTS_DEV, SETS * DEAL_PAD), jnp.bfloat16),
        ),
        in_specs=[SMEM] + [VMEM] * 4,
        out_specs=(VMEM,) * 2,
        compiler_params=pltpu.CompilerParams(vmem_limit_bytes=8 << 20),
        cost_estimate=pl.CostEstimate(flops=1 << 30, bytes_accessed=1 << 20, transcendentals=0),
    )(here, code, rank, own, at)
    moved = moved.astype(jnp.int32)
    rows = jnp.arange(QUARTERS * GROUP)
    pick, other = (
        (rows[:, None] + 1 == (moved[:, 2 * i] * 32 + moved[:, 2 * i + 1]).reshape(1, -1)).astype(
            jnp.bfloat16
        )
        for i in range(2)
    )

    both = jnp.concatenate([pick, other])
    n_rows = QUARTERS * GROUP
    soon = jnp.dot(
        both[:, : 5 * SEND], jnp.concatenate(chunks[:5]), preferred_element_type=jnp.float32
    ).astype(jnp.bfloat16)
    soon, *middle = lax.optimization_barrier((soon, *chunks[5:7]))
    soon = jnp.dot(
        both[:, 5 * SEND : 7 * SEND],
        jnp.concatenate(middle),
        preferred_element_type=jnp.float32,
    ).astype(jnp.bfloat16) + soon
    soon = lax.optimization_barrier(soon)
    early_b = lax.ppermute(soon[n_rows:], "core", SWAP)
    late_b = lax.ppermute(chunks[-1], "core", SWAP)
    late = pick[:, 7 * SEND :]
    x = jnp.concatenate(
        [
            early + jnp.dot(late, rest, preferred_element_type=jnp.float32).astype(jnp.bfloat16)
            for early, rest in ((soon[:n_rows], chunks[-1]), (early_b, late_b))
        ],
        axis=1,
    )

    keeps, gots = [], []
    for part in range(2):
        some = slice(2 * part, 2 * part + 2)
        keep, give = product(x, near[some], far[some])
        keeps.append(keep)
        gots.append(lax.ppermute(give, "x_hi", SWAP))
    hidden = pl.pallas_call(
        gated_kernel,
        out_shape=jax.ShapeDtypeStruct((2 * HALVES * SETS, SETS, DEAL_PAD, LANES), jnp.bfloat16),
        in_specs=[SMEM] + [VMEM] * 4,
        out_specs=VMEM,
        compiler_params=pltpu.CompilerParams(vmem_limit_bytes=16 << 20),
        cost_estimate=pl.CostEstimate(flops=1 << 30, bytes_accessed=1 << 22, transcendentals=0),
    )(here, *keeps, *gots)
    hidden = lax.all_to_all(hidden, ("x_lo", "y", "core"), 0, 0)
    return pl.pallas_call(
        placed_kernel,
        out_shape=jax.ShapeDtypeStruct((2, SLOTS_DEV, HALVES * SETS * LANES), jnp.bfloat16),
        in_specs=[VMEM] * 2,
        out_specs=VMEM,
        compiler_params=pltpu.CompilerParams(vmem_limit_bytes=8 << 20),
        cost_estimate=pl.CostEstimate(flops=1 << 28, bytes_accessed=1 << 20, transcendentals=0),
    )(hidden, places)


def solution(mesh):
    cut = jax.sharding.Mesh(
        mesh.devices.reshape(ROWS, HALVES, SETS, 2, 2), ("z", "x_lo", "y", "x_hi", "core")
    )
    layer, col = ("x_hi", "core"), ("x_lo", "y")
    in_specs = (P("z", layer), P(), P(None, layer, ("z", *col)), P(None, layer, ("z", *col)))
    out_specs = P(None, (*col, *layer), "z")
    return jax.shard_map(shards, mesh=cut, in_specs=in_specs, out_specs=out_specs, check_vma=False)
```

time: 270 us -> 159 us (0.59)
  waiting for transfers between devices: 152 us -> 76.6 us
  local copies, waits for them, and re-layouts: 80.4 us -> 7.66 us
  starting transfers between devices: 0.31 us -> 32.9 us
  between operations: 15 us -> 0.26 us
  blocking collectives: 0 us -> 14.2 us
  Pallas kernels: 0 us -> 11.9 us
  other arithmetic: 12.1 us -> 2.79 us
    all_gather x2 -> x0, waiting for transfers between devices: 88.9 us -> none  [on_gathered_pieces(): done.append(jax.vmap(apply)(lax.all_gather(piece, axis), starts))]
    ppermute x0 -> x19, waiting for transfers between devices: none -> 76.6 us  [the longest x3 20.6 us: rows_of_ring(): up = lax.ppermute(up, 'z', z_perm(1))]
    reduce_scatter x1 -> x0, waiting for transfers between devices: 62 us -> none  [shards(): parts = lax.psum_scatter(totals, 'layer', scatter_dimension=2, tiled=True)]
    unnamed x18 -> x17, local copies, waits for them, and re-layouts: 46.3 us -> 3.65 us
    ppermute x0 -> x19, starting transfers between devices: none -> 32.9 us  [the longest x3 9.71 us: rows_of_ring(): down = lax.ppermute(down, 'z', z_perm(-1))]
    all_to_all x0 -> x1, blocking collectives: none -> 14.2 us  [shards(): hidden = lax.all_to_all(hidden, ('x_lo', 'y', 'core'), 0, 0)]
    all_gather x2 -> x0, local copies, waits for them, and re-layouts: 12.2 us -> none  [on_gathered_pieces(): done.append(jax.vmap(apply)(lax.all_gather(piece, axis), starts))]
    pallas_call x0 -> x6, Pallas kernels: none -> 11.9 us  [the longest x2 5.16 us: product(): pl.pallas_call(product_kernel, out_shape=(jax.ShapeDtypeStruct((rows // 2...]
  transfers between devices with their start and end apart: 4 -> 19, of which waited for: 3 -> 11; matrix products, arithmetic and copies ran while one was open for 26% -> 9% of each run, Pallas kernels for 0% -> 5%
where the time goes in v1:
time: 159 us
  waiting for transfers between devices  76.6 us (48%)
  starting transfers between devices  32.9 us (21%)
  blocking collectives  14.2 us (9%)
  matrix products  12.3 us (8%)
  Pallas kernels  11.9 us (7%)
  local copies, waits for them, and re-layouts  7.66 us (5%)
  other arithmetic  2.79 us (2%)
    ppermute x3, waiting for transfers between devices, rows_of_ring(): up = lax.ppermute(up, 'z', z_perm(1))  20.6 us
    ppermute x1, waiting for transfers between devices, weights_of_ring(): near3 = lax.ppermute(near1, 'y', y_perm(1))  20.6 us
    all_to_all x1, blocking collectives, shards(): hidden = lax.all_to_all(hidden, ('x_lo', 'y', 'core'), 0, 0)  14.2 us
    ppermute x2, waiting for transfers between devices, shards(): gots.append(lax.ppermute(give, 'x_hi', SWAP))  12.7 us
    ppermute x1, waiting for transfers between devices, weights_of_ring(): near2 = lax.ppermute(near, 'y', y_perm(-1))  10.3 us
    ppermute x3, starting transfers between devices, rows_of_ring(): down = lax.ppermute(down, 'z', z_perm(-1))  9.71 us
    dot_general x1, matrix products, shards(): jnp.dot(both[:, :5 * SEND], jnp.concatenate(chunks[:5]), preferred_elemen...  6.66 us
    ppermute x1, waiting for transfers between devices, weights_of_ring(): near1 = lax.ppermute(near, 'y', y_perm(1))  5.6 us
  transfers between devices with their start and end apart: 19, of which 11 were waited for; matrix products, arithmetic and copies ran while one was open for 9% of the time, Pallas kernels for 5%

profile of v1, /device:TPU:1, one launch (start us, length us, event | category | flops | bytes accessed | tf_op | source)
XLA Modules:
  0.0 158.6 jit_solution(15439654177584537908)
XLA Ops:
  1.0 1.5 copy-done
  2.6 1.7 %shard_map.46 = (bf16[168,1536]{1,0:T(8,128)(2,1)S(1)}, s32[3,40,128]{2,1,0:T(8,128)S(1)}, s32[40,128]{1,0:T(8,128)S(1)}, s32[8,8,128]{2,1,0:T(8,128)S(1)}) custom-call(s32[5]{0:T(128)S(1)} %stack.33.here, s32[40,128]{1,0:T(8,128)S(1)} %add_bitcast_fusion.code, bf16[640,1536]{1,0:T(8,128)(2,1)S(1)} %copy-done), custom_call_target="tpu_custom_call" | custom-call | flops 1073741824 | bytes 4194304 | tf_op jit(solution)/shard_map/pallas_call | solution.py:286
  4.3 2.5 %collective-permute-start = (bf16[168,1536]{1,0:T(8,128)(2,1)S(1)}, bf16[168,1536]{1,0:T(8,128)(2,1)S(1)}, u32[]{:S(2)}, u32[]{:S(2)}) collective-permute-start(bf16[168,1536]{1,0:T(8,128)(2,1)S(1)} %get-tuple-element.22), channel_id=1, source_target_pairs={{0,32},{32,64},{64,96},{96,128},{128,160},{160,192},{192,224},{224... | collective-permute-start | bytes 1548296 | tf_op jit(solution)/shard_map/ppermute | solution.py:61
  6.8 4.0 %collective-permute-start.1 = (bf16[168,1536]{1,0:T(8,128)(2,1)S(1)}, bf16[168,1536]{1,0:T(8,128)(2,1)S(1)}, u32[]{:S(2)}, u32[]{:S(2)}) collective-permute-start(bf16[168,1536]{1,0:T(8,128)(2,1)S(1)} %get-tuple-element.22), channel_id=1, source_target_pairs={{0,224},{32,0},{64,32},{96,64},{128,96},{160,128},{192,160},{224,1... | collective-permute-start | bytes 1548296 | tf_op jit(solution)/shard_map/ppermute | solution.py:62
  10.9 2.5 %shard_map.47 = (f32[8,8,168]{2,1,0:T(8,128)S(1)}, bf16[2,80,96]{2,1,0:T(8,128)(2,1)S(1)}) custom-call(s32[5]{0:T(128)S(1)} %stack.33.here, s32[40,128]{1,0:T(8,128)S(1)} %add_bitcast_fusion.code, s32[3,40,128]{2,1,0:T(8,128)S(1)} %get-tuple-element.18.rank, s32[40,128]{1,0:T(8,128)S(1)} %get-tuple-element.19.own, s32[8,8,128]{2,1,0:T(8,128)S(1)} %get-tuple-element.20.at), custom_call_target="tpu_custom_call" | custom-call | flops 1073741824 | bytes 1048576 | tf_op jit(solution)/shard_map/pallas_call | solution.py:301
  14.7 7.5 %collective-permute-done = bf16[168,1536]{1,0:T(8,128)(2,1)S(1)} collective-permute-done((bf16[168,1536]{1,0:T(8,128)(2,1)S(1)}, bf16[168,1536]{1,0:T(8,128)(2,1)S(1)}, u32[]{:S(2)}, u32[]{:S(2)}) %collective-permute-start) | collective-permute-done | bytes 516128 | tf_op jit(solution)/shard_map/ppermute | solution.py:61
  22.3 2.7 %collective-permute-start.3 = (bf16[168,1536]{1,0:T(8,128)(2,1)S(1)}, bf16[168,1536]{1,0:T(8,128)(2,1)S(1)}, u32[]{:S(2)}, u32[]{:S(2)}) collective-permute-start(bf16[168,1536]{1,0:T(8,128)(2,1)S(1)} %collective-permute-done.1), channel_id=1, source_target_pairs={{0,224},{32,0},{64,32},{96,64},{128,96},{160,128},{192,160},{224,1... | collective-permute-start | bytes 1548296 | tf_op jit(solution)/shard_map/ppermute | solution.py:62
  25.1 10.4 %collective-permute-done.2 = bf16[168,1536]{1,0:T(8,128)(2,1)S(1)} collective-permute-done((bf16[168,1536]{1,0:T(8,128)(2,1)S(1)}, bf16[168,1536]{1,0:T(8,128)(2,1)S(1)}, u32[]{:S(2)}, u32[]{:S(2)}) %collective-permute-start.2) | collective-permute-done | bytes 516128 | tf_op jit(solution)/shard_map/ppermute | solution.py:61
  35.5 2.9 %collective-permute-start.5 = (bf16[168,1536]{1,0:T(8,128)(2,1)S(1)}, bf16[168,1536]{1,0:T(8,128)(2,1)S(1)}, u32[]{:S(2)}, u32[]{:S(2)}) collective-permute-start(bf16[168,1536]{1,0:T(8,128)(2,1)S(1)} %collective-permute-done.3), channel_id=1, source_target_pairs={{0,224},{32,0},{64,32},{96,64},{128,96},{160,128},{192,160},{224,1... | collective-permute-start | bytes 1548296 | tf_op jit(solution)/shard_map/ppermute | solution.py:62
  38.5 6.7 %convolution_convert_fusion.1 = bf16[1344,1536]{1,0:T(8,128)(2,1)S(1)} fusion(bf16[840,1536]{1,0:T(8,128)(2,1)S(1)} %constant_dynamic-update-slice_fusion, pred[672,1344]{1,0:T(32,128)(4,1)S(1)} %get-tuple-element.40, pred[672,1344]{1,0:T(32,128)(4,1)S(1)} %get-tuple-element.39), kind=kOutput, calls=%fused_computation.1 | convolution fusion | flops 3471358464 | bytes 8515584 | tf_op jit(solution)/shard_map/dot_general | solution.py:323
  45.2 2.7 %collective-permute-done.4 = bf16[168,1536]{1,0:T(8,128)(2,1)S(1)} collective-permute-done((bf16[168,1536]{1,0:T(8,128)(2,1)S(1)}, bf16[168,1536]{1,0:T(8,128)(2,1)S(1)}, u32[]{:S(2)}, u32[]{:S(2)}) %collective-permute-start.4) | collective-permute-done | bytes 516128 | tf_op jit(solution)/shard_map/ppermute | solution.py:61
  47.9 2.4 %fusion.7 = bf16[1344,1536]{1,0:T(8,128)(2,1)S(1)} fusion(bf16[1344,1536]{1,0:T(8,128)(2,1)S(1)} %convolution_convert_fusion.1, pred[672,1344]{1,0:T(32,128)(4,1)S(1)} %get-tuple-element.40, pred[672,1344]{1,0:T(32,128)(4,1)S(1)} %get-tuple-element.39, bf16[168,1536]{1,0:T(8,128)(2,1)S(1)} %collective-permute-done.5, ...), kind=kOutput, calls=%fused_computation.15 | convolution fusion | flops 1393910784 | bytes 11096064 | tf_op jit(solution)/shard_map/dot_general | solution.py:327
  50.3 1.9 %copy-done.2 = bf16[1344,1536]{1,0:T(8,128)(2,1)} copy-done((bf16[1344,1536]{1,0:T(8,128)(2,1)}, bf16[1344,1536]{1,0:T(8,128)(2,1)S(1)}, u32[]{:S(2)}) %copy-start.2) | copy-done | bytes 4128792
  53.7 3.0 %collective-permute-start.8 = (bf16[672,1536]{1,0:T(8,128)(2,1)}, bf16[672,1536]{1,0:T(8,128)(2,1)S(1)}, u32[]{:S(2)}, u32[]{:S(2)}) collective-permute-start(bf16[672,1536]{1,0:T(8,128)(2,1)} %slice.52), channel_id=1, source_target_pairs={{0,1},{1,0},{2,3},{3,2},{4,5},{5,4},{6,7},{7,6},{8,9},{9,8},{10,11... | collective-permute-start | bytes 6193160 | tf_op jit(solution)/shard_map/ppermute | solution.py:333
  60.5 3.0 %collective-permute-start.7 = (bf16[80,1536]{1,0:T(8,128)(2,1)S(1)}, bf16[80,1536]{1,0:T(8,128)(2,1)S(1)}, u32[]{:S(2)}, u32[]{:S(2)}) collective-permute-start(bf16[80,1536]{1,0:T(8,128)(2,1)S(1)} %slice.51), channel_id=1, source_target_pairs={{0,224},{32,0},{64,32},{96,64},{128,96},{160,128},{192,160},{224,1... | collective-permute-start | bytes 737288 | tf_op jit(solution)/shard_map/ppermute | solution.py:66
  63.6 2.2 %collective-permute-start.15 = (bf16[2,1536,128]{2,1,0:T(8,128)(2,1)S(1)}, bf16[2,1536,128]{2,1,0:T(8,128)(2,1)S(1)}, u32[]{:S(2)}, u32[]{:S(2)}) collective-permute-start(bf16[2,1536,128]{2,1,0:T(8,128)(2,1)S(1)} %pad_maximum_fusion.2), channel_id=1, source_target_pairs={{0,13},{1,12},{4,1},{5,0},{8,5},{9,4},{12,9},{13,8},{2,15},{3,14},... | collective-permute-start | bytes 2359304 | tf_op jit(solution)/shard_map/ppermute | solution.py:49
  65.8 2.1 %collective-permute-done.6 = bf16[88,1536]{1,0:T(8,128)(2,1)S(1)} collective-permute-done((bf16[88,1536]{1,0:T(8,128)(2,1)S(1)}, bf16[88,1536]{1,0:T(8,128)(2,1)S(1)}, u32[]{:S(2)}, u32[]{:S(2)}) %collective-permute-start.6) | collective-permute-done | bytes 270368 | tf_op jit(solution)/shard_map/ppermute | solution.py:65
  69.8 1.6 %collective-permute-start.13 = (bf16[2,1536,128]{2,1,0:T(8,128)(2,1)S(1)}, bf16[2,1536,128]{2,1,0:T(8,128)(2,1)S(1)}, u32[]{:S(2)}, u32[]{:S(2)}) collective-permute-start(bf16[2,1536,128]{2,1,0:T(8,128)(2,1)S(1)} %pad_maximum_fusion.1.refs_0_), channel_id=1, source_target_pairs={{0,12},{4,0},{8,4},{12,8},{1,13},{5,1},{9,5},{13,9},{2,14},{6,2},{... | collective-permute-start | bytes 2359304 | tf_op jit(solution)/shard_map/ppermute | solution.py:51
  71.4 1.6 %fusion.1 = bf16[672,1536]{1,0:T(8,128)(2,1)S(1)} fusion(bf16[168,1536]{1,0:T(8,128)(2,1)S(1)} %constant_dynamic-update-slice_fusion.5, bf16[1344,1536]{1,0:T(8,128)(2,1)S(1)} %copy-done.3, pred[672,1344]{1,0:T(32,128)(4,1)} %copy-done.1), kind=kOutput, calls=%fused_computation.7 | convolution fusion | flops 348880896 | bytes 4816896 | tf_op jit(solution)/shard_map/dot_general | solution.py:338
  73.1 5.6 %collective-permute-done.10.refs_1_ = bf16[2,1536,128]{2,1,0:T(8,128)(2,1)S(1)} collective-permute-done((bf16[2,1536,128]{2,1,0:T(8,128)(2,1)S(1)}, bf16[2,1536,128]{2,1,0:T(8,128)(2,1)S(1)}, u32[]{:S(2)}, u32[]{:S(2)}) %collective-permute-start.10) | collective-permute-done | bytes 786464 | tf_op jit(solution)/shard_map/ppermute | solution.py:48
  79.5 4.1 %collective-permute-done.15.refs_2_ = bf16[2,1536,128]{2,1,0:T(8,128)(2,1)S(1)} collective-permute-done((bf16[2,1536,128]{2,1,0:T(8,128)(2,1)S(1)}, bf16[2,1536,128]{2,1,0:T(8,128)(2,1)S(1)}, u32[]{:S(2)}, u32[]{:S(2)}) %collective-permute-start.15) | collective-permute-done | bytes 786464 | tf_op jit(solution)/shard_map/ppermute | solution.py:49
  83.6 1.6 collective-permute-start.12
  86.2 1.7 %collective-permute-start.16 = (bf16[2,1536,128]{2,1,0:T(8,128)(2,1)S(1)}, bf16[2,1536,128]{2,1,0:T(8,128)(2,1)S(1)}, u32[]{:S(2)}, u32[]{:S(2)}) collective-permute-start(bf16[2,1536,128]{2,1,0:T(8,128)(2,1)S(1)} %collective-permute-done.15.refs_2_), channel_id=1, source_target_pairs={{0,12},{4,0},{8,4},{12,8},{1,13},{5,1},{9,5},{13,9},{2,14},{6,2},{... | collective-permute-start | bytes 2359304 | tf_op jit(solution)/shard_map/ppermute | solution.py:54
  87.9 1.6 %fusion.2 = bf16[672,1536]{1,0:T(8,128)(2,1)S(1)} fusion(bf16[672,1536]{1,0:T(8,128)(2,1)S(1)} %collective-permute-done.8, bf16[168,1536]{1,0:T(8,128)(2,1)S(1)} %collective-permute-done.9, pred[672,1344]{1,0:T(32,128)(4,1)} %copy-done.1), kind=kOutput, calls=%fused_computation.8 | convolution fusion | flops 348880896 | bytes 4816896 | tf_op jit(solution)/shard_map/dot_general | solution.py:338
  90.1 10.3 %collective-permute-done.13.refs_0_ = bf16[2,1536,128]{2,1,0:T(8,128)(2,1)S(1)} collective-permute-done((bf16[2,1536,128]{2,1,0:T(8,128)(2,1)S(1)}, bf16[2,1536,128]{2,1,0:T(8,128)(2,1)S(1)}, u32[]{:S(2)}, u32[]{:S(2)}) %collective-permute-start.13) | collective-permute-done | bytes 786464 | tf_op jit(solution)/shard_map/ppermute | solution.py:51
  100.4 20.6 %collective-permute-done.14.refs_1_ = bf16[2,1536,128]{2,1,0:T(8,128)(2,1)S(1)} collective-permute-done((bf16[2,1536,128]{2,1,0:T(8,128)(2,1)S(1)}, bf16[2,1536,128]{2,1,0:T(8,128)(2,1)S(1)}, u32[]{:S(2)}, u32[]{:S(2)}) %collective-permute-start.14) | collective-permute-done | bytes 786464 | tf_op jit(solution)/shard_map/ppermute | solution.py:53
  121.0 2.6 %shard_map.49 = (f32[336,512]{1,0:T(8,128)S(1)}, s16[352,512]{1,0:T(8,128)(2,1)S(1)}) custom-call(bf16[672,3072]{1,0:T(8,128)(2,1)S(1)} %pad_maximum_fusion.x, bf16[2,1536,128]{2,1,0:T(8,128)(2,1)S(1)} %collective-permute-done.13.refs_0_, bf16[2,1536,128]{2,1,0:T(8,128)(2,1)S(1)} %collective-permute-done.14.refs_1_, ...), custom_call_target="tpu_custom_call" | custom-call | flops 2113929216 | bytes 8650752 | tf_op jit(solution)/shard_map/pallas_call | solution.py:221
  123.6 2.8 %collective-permute-start.18 = (s16[352,512]{1,0:T(8,128)(2,1)S(1)}, s16[352,512]{1,0:T(8,128)(2,1)S(1)}, u32[]{:S(2)}, u32[]{:S(2)}) collective-permute-start(s16[352,512]{1,0:T(8,128)(2,1)S(1)} %get-tuple-element.29), channel_id=1, source_target_pairs={{0,2},{2,0},{1,3},{3,1},{4,6},{6,4},{5,7},{7,5},{8,10},{10,8},{9,1... | collective-permute-start | bytes 1081352 | tf_op jit(solution)/shard_map/ppermute | solution.py:349
  126.4 2.6 %shard_map.48 = (f32[336,512]{1,0:T(8,128)S(1)}, s16[352,512]{1,0:T(8,128)(2,1)S(1)}) custom-call(bf16[672,3072]{1,0:T(8,128)(2,1)S(1)} %pad_maximum_fusion.x, bf16[2,1536,128]{2,1,0:T(8,128)(2,1)S(1)} %pad_maximum_fusion.1.refs_0_, bf16[2,1536,128]{2,1,0:T(8,128)(2,1)S(1)} %collective-permute-done.10.refs_1_, ...), custom_call_target="tpu_custom_call" | custom-call | flops 2113929216 | bytes 8650752 | tf_op jit(solution)/shard_map/pallas_call | solution.py:221
  129.3 4.9 %collective-permute-done.18.refs_3_ = s16[352,512]{1,0:T(8,128)(2,1)S(1)} collective-permute-done((s16[352,512]{1,0:T(8,128)(2,1)S(1)}, s16[352,512]{1,0:T(8,128)(2,1)S(1)}, u32[]{:S(2)}, u32[]{:S(2)}) %collective-permute-start.18) | collective-permute-done | bytes 360480 | tf_op jit(solution)/shard_map/ppermute | solution.py:349
  134.3 7.7 %collective-permute-done.17.refs_2_ = s16[352,512]{1,0:T(8,128)(2,1)S(1)} collective-permute-done((s16[352,512]{1,0:T(8,128)(2,1)S(1)}, s16[352,512]{1,0:T(8,128)(2,1)S(1)}, u32[]{:S(2)}, u32[]{:S(2)}) %collective-permute-start.17) | collective-permute-done | bytes 360480 | tf_op jit(solution)/shard_map/ppermute | solution.py:349
  143.5 14.2 %all_to_all.5.got = bf16[16,4,24,128]{3,2,1,0:T(8,128)(2,1)S(1)} all-to-all(bf16[16,4,24,128]{3,2,1,0:T(8,128)(2,1)S(1)} %shard_map.50), channel_id=1, replica_groups=mesh['z'=8,'x_lo'=2,'y'=4,'x_hi'=2,'core'=2] {'x_lo','y','core'}, dimensions={0} | all-to-all | bytes 786432 | tf_op jit(solution)/shard_map/all_to_all | solution.py:358
  (52 shorter events, 14.9 us)
Async XLA Ops:
  1.0 1.5 copy-start
  4.3 17.9 %collective-permute-start = (bf16[168,1536]{1,0:T(8,128)(2,1)S(1)}, bf16[168,1536]{1,0:T(8,128)(2,1)S(1)}, u32[]{:S(2)}, u32[]{:S(2)}) collective-permute-start(bf16[168,1536]{1,0:T(8,128)(2,1)S(1)} %get-tuple-element.22), channel_id=1, source_target_pairs={{0,32},{32,64},{64,96},{96,128},{128,160},{160,192},{192,224},{224... | collective-permute-start | bytes 1548296 | tf_op jit(solution)/shard_map/ppermute | solution.py:61
  6.8 15.4 %collective-permute-start.1 = (bf16[168,1536]{1,0:T(8,128)(2,1)S(1)}, bf16[168,1536]{1,0:T(8,128)(2,1)S(1)}, u32[]{:S(2)}, u32[]{:S(2)}) collective-permute-start(bf16[168,1536]{1,0:T(8,128)(2,1)S(1)} %get-tuple-element.22), channel_id=1, source_target_pairs={{0,224},{32,0},{64,32},{96,64},{128,96},{160,128},{192,160},{224,1... | collective-permute-start | bytes 1548296 | tf_op jit(solution)/shard_map/ppermute | solution.py:62
  14.7 33.2 %copy-start.1 = (pred[672,1344]{1,0:T(32,128)(4,1)}, pred[672,1344]{1,0:T(32,128)(4,1)S(1)}, u32[]{:S(2)}) copy-start(pred[672,1344]{1,0:T(32,128)(4,1)S(1)} %get-tuple-element.39) | copy-start | bytes 2709508
  22.2 13.3 %collective-permute-start.2 = (bf16[168,1536]{1,0:T(8,128)(2,1)S(1)}, bf16[168,1536]{1,0:T(8,128)(2,1)S(1)}, u32[]{:S(2)}, u32[]{:S(2)}) collective-permute-start(bf16[168,1536]{1,0:T(8,128)(2,1)S(1)} %collective-permute-done), channel_id=1, source_target_pairs={{0,32},{32,64},{64,96},{96,128},{128,160},{160,192},{192,224},{224... | collective-permute-start | bytes 1548296 | tf_op jit(solution)/shard_map/ppermute | solution.py:61
  22.3 13.3 %collective-permute-start.3 = (bf16[168,1536]{1,0:T(8,128)(2,1)S(1)}, bf16[168,1536]{1,0:T(8,128)(2,1)S(1)}, u32[]{:S(2)}, u32[]{:S(2)}) collective-permute-start(bf16[168,1536]{1,0:T(8,128)(2,1)S(1)} %collective-permute-done.1), channel_id=1, source_target_pairs={{0,224},{32,0},{64,32},{96,64},{128,96},{160,128},{192,160},{224,1... | collective-permute-start | bytes 1548296 | tf_op jit(solution)/shard_map/ppermute | solution.py:62
  35.5 12.4 %collective-permute-start.4 = (bf16[168,1536]{1,0:T(8,128)(2,1)S(1)}, bf16[168,1536]{1,0:T(8,128)(2,1)S(1)}, u32[]{:S(2)}, u32[]{:S(2)}) collective-permute-start(bf16[168,1536]{1,0:T(8,128)(2,1)S(1)} %collective-permute-done.2), channel_id=1, source_target_pairs={{0,32},{32,64},{64,96},{96,128},{128,160},{160,192},{192,224},{224... | collective-permute-start | bytes 1548296 | tf_op jit(solution)/shard_map/ppermute | solution.py:61
  35.5 12.4 %collective-permute-start.5 = (bf16[168,1536]{1,0:T(8,128)(2,1)S(1)}, bf16[168,1536]{1,0:T(8,128)(2,1)S(1)}, u32[]{:S(2)}, u32[]{:S(2)}) collective-permute-start(bf16[168,1536]{1,0:T(8,128)(2,1)S(1)} %collective-permute-done.3), channel_id=1, source_target_pairs={{0,224},{32,0},{64,32},{96,64},{128,96},{160,128},{192,160},{224,1... | collective-permute-start | bytes 1548296 | tf_op jit(solution)/shard_map/ppermute | solution.py:62
  47.9 2.4 %copy-start.5 = (bf16[168,1536]{1,0:T(8,128)(2,1)}, bf16[168,1536]{1,0:T(8,128)(2,1)S(1)}, u32[]{:S(2)}) copy-start(bf16[168,1536]{1,0:T(8,128)(2,1)S(1)} %collective-permute-done.5) | copy-start | bytes 1548292
  50.3 1.9 %copy-start.2 = (bf16[1344,1536]{1,0:T(8,128)(2,1)}, bf16[1344,1536]{1,0:T(8,128)(2,1)S(1)}, u32[]{:S(2)}) copy-start(bf16[1344,1536]{1,0:T(8,128)(2,1)S(1)} %fusion.7) | copy-start | bytes 12386308
  52.3 4.4 %copy-start.4 = (bf16[2,1536,128]{2,1,0:T(8,128)(2,1)S(1)}, bf16[2,1536,128]{2,1,0:T(8,128)(2,1)}, u32[]{:S(2)}) copy-start(bf16[2,1536,128]{2,1,0:T(8,128)(2,1)} %param.7) | copy-start | bytes 2359300
  53.7 32.4 %collective-permute-start.8 = (bf16[672,1536]{1,0:T(8,128)(2,1)}, bf16[672,1536]{1,0:T(8,128)(2,1)S(1)}, u32[]{:S(2)}, u32[]{:S(2)}) collective-permute-start(bf16[672,1536]{1,0:T(8,128)(2,1)} %slice.52), channel_id=1, source_target_pairs={{0,1},{1,0},{2,3},{3,2},{4,5},{5,4},{6,7},{7,6},{8,9},{9,8},{10,11... | collective-permute-start | bytes 6193160 | tf_op jit(solution)/shard_map/ppermute | solution.py:333
  58.0 13.5 %copy-start.3 = (bf16[1344,1536]{1,0:T(8,128)(2,1)S(1)}, bf16[1344,1536]{1,0:T(8,128)(2,1)}, u32[]{:S(2)}) copy-start(bf16[1344,1536]{1,0:T(8,128)(2,1)} %copy-done.2) | copy-start | bytes 12386308
  58.0 9.9 %collective-permute-start.6 = (bf16[88,1536]{1,0:T(8,128)(2,1)S(1)}, bf16[88,1536]{1,0:T(8,128)(2,1)S(1)}, u32[]{:S(2)}, u32[]{:S(2)}) collective-permute-start(bf16[88,1536]{1,0:T(8,128)(2,1)S(1)} %slice.50), channel_id=1, source_target_pairs={{0,32},{32,64},{64,96},{96,128},{128,160},{160,192},{192,224},{224... | collective-permute-start | bytes 811016 | tf_op jit(solution)/shard_map/ppermute | solution.py:65
  58.2 20.5 %collective-permute-start.10 = (bf16[2,1536,128]{2,1,0:T(8,128)(2,1)S(1)}, bf16[2,1536,128]{2,1,0:T(8,128)(2,1)S(1)}, u32[]{:S(2)}, u32[]{:S(2)}) collective-permute-start(bf16[2,1536,128]{2,1,0:T(8,128)(2,1)S(1)} %pad_maximum_fusion.1.refs_0_), channel_id=1, source_target_pairs={{0,4},{4,8},{8,12},{12,0},{1,5},{5,9},{9,13},{13,1},{2,6},{6,10},{... | collective-permute-start | bytes 2359304 | tf_op jit(solution)/shard_map/ppermute | solution.py:48
  60.5 8.1 %collective-permute-start.7 = (bf16[80,1536]{1,0:T(8,128)(2,1)S(1)}, bf16[80,1536]{1,0:T(8,128)(2,1)S(1)}, u32[]{:S(2)}, u32[]{:S(2)}) collective-permute-start(bf16[80,1536]{1,0:T(8,128)(2,1)S(1)} %slice.51), channel_id=1, source_target_pairs={{0,224},{32,0},{64,32},{96,64},{128,96},{160,128},{192,160},{224,1... | collective-permute-start | bytes 737288 | tf_op jit(solution)/shard_map/ppermute | solution.py:66
  63.6 20.0 %collective-permute-start.15 = (bf16[2,1536,128]{2,1,0:T(8,128)(2,1)S(1)}, bf16[2,1536,128]{2,1,0:T(8,128)(2,1)S(1)}, u32[]{:S(2)}, u32[]{:S(2)}) collective-permute-start(bf16[2,1536,128]{2,1,0:T(8,128)(2,1)S(1)} %pad_maximum_fusion.2), channel_id=1, source_target_pairs={{0,13},{1,12},{4,1},{5,0},{8,5},{9,4},{12,9},{13,8},{2,15},{3,14},... | collective-permute-start | bytes 2359304 | tf_op jit(solution)/shard_map/ppermute | solution.py:49
  68.6 16.6 %collective-permute-start.9 = (bf16[168,1536]{1,0:T(8,128)(2,1)S(1)}, bf16[168,1536]{1,0:T(8,128)(2,1)S(1)}, u32[]{:S(2)}, u32[]{:S(2)}) collective-permute-start(bf16[168,1536]{1,0:T(8,128)(2,1)S(1)} %constant_dynamic-update-slice_fusion.5), channel_id=1, source_target_pairs={{0,1},{1,0},{2,3},{3,2},{4,5},{5,4},{6,7},{7,6},{8,9},{9,8},{10,11... | collective-permute-start | bytes 1548296 | tf_op jit(solution)/shard_map/ppermute | solution.py:334
  69.8 30.6 %collective-permute-start.13 = (bf16[2,1536,128]{2,1,0:T(8,128)(2,1)S(1)}, bf16[2,1536,128]{2,1,0:T(8,128)(2,1)S(1)}, u32[]{:S(2)}, u32[]{:S(2)}) collective-permute-start(bf16[2,1536,128]{2,1,0:T(8,128)(2,1)S(1)} %pad_maximum_fusion.1.refs_0_), channel_id=1, source_target_pairs={{0,12},{4,0},{8,4},{12,8},{1,13},{5,1},{9,5},{13,9},{2,14},{6,2},{... | collective-permute-start | bytes 2359304 | tf_op jit(solution)/shard_map/ppermute | solution.py:51
  78.7 47.7 %collective-permute-start.11 = (bf16[2,1536,128]{2,1,0:T(8,128)(2,1)S(1)}, bf16[2,1536,128]{2,1,0:T(8,128)(2,1)S(1)}, u32[]{:S(2)}, u32[]{:S(2)}) collective-permute-start(bf16[2,1536,128]{2,1,0:T(8,128)(2,1)S(1)} %pad_maximum_fusion.2), channel_id=1, source_target_pairs={{0,1},{1,0},{2,3},{3,2},{4,5},{5,4},{6,7},{7,6},{8,9},{9,8},{10,11... | collective-permute-start | bytes 2359304 | tf_op jit(solution)/shard_map/ppermute | solution.py:52
  83.6 42.8 %collective-permute-start.12 = (bf16[2,1536,128]{2,1,0:T(8,128)(2,1)S(1)}, bf16[2,1536,128]{2,1,0:T(8,128)(2,1)S(1)}, u32[]{:S(2)}, u32[]{:S(2)}) collective-permute-start(bf16[2,1536,128]{2,1,0:T(8,128)(2,1)S(1)} %pad_maximum_fusion.2), channel_id=1, source_target_pairs={{0,5},{1,4},{4,9},{5,8},{8,13},{9,12},{12,1},{13,0},{2,7},{3,6},{6... | collective-permute-start | bytes 2359304 | tf_op jit(solution)/shard_map/ppermute | solution.py:50
  85.2 35.8 %collective-permute-start.14 = (bf16[2,1536,128]{2,1,0:T(8,128)(2,1)S(1)}, bf16[2,1536,128]{2,1,0:T(8,128)(2,1)S(1)}, u32[]{:S(2)}, u32[]{:S(2)}) collective-permute-start(bf16[2,1536,128]{2,1,0:T(8,128)(2,1)S(1)} %collective-permute-done.10.refs_1_), channel_id=1, source_target_pairs={{0,4},{4,8},{8,12},{12,0},{1,5},{5,9},{9,13},{13,1},{2,6},{6,10},{... | collective-permute-start | bytes 2359304 | tf_op jit(solution)/shard_map/ppermute | solution.py:53
  86.2 34.8 %collective-permute-start.16 = (bf16[2,1536,128]{2,1,0:T(8,128)(2,1)S(1)}, bf16[2,1536,128]{2,1,0:T(8,128)(2,1)S(1)}, u32[]{:S(2)}, u32[]{:S(2)}) collective-permute-start(bf16[2,1536,128]{2,1,0:T(8,128)(2,1)S(1)} %collective-permute-done.15.refs_2_), channel_id=1, source_target_pairs={{0,12},{4,0},{8,4},{12,8},{1,13},{5,1},{9,5},{13,9},{2,14},{6,2},{... | collective-permute-start | bytes 2359304 | tf_op jit(solution)/shard_map/ppermute | solution.py:54
  123.6 10.7 %collective-permute-start.18 = (s16[352,512]{1,0:T(8,128)(2,1)S(1)}, s16[352,512]{1,0:T(8,128)(2,1)S(1)}, u32[]{:S(2)}, u32[]{:S(2)}) collective-permute-start(s16[352,512]{1,0:T(8,128)(2,1)S(1)} %get-tuple-element.29), channel_id=1, source_target_pairs={{0,2},{2,0},{1,3},{3,1},{4,6},{6,4},{5,7},{7,5},{8,10},{10,8},{9,1... | collective-permute-start | bytes 1081352 | tf_op jit(solution)/shard_map/ppermute | solution.py:349
  129.0 13.0 %collective-permute-start.17 = (s16[352,512]{1,0:T(8,128)(2,1)S(1)}, s16[352,512]{1,0:T(8,128)(2,1)S(1)}, u32[]{:S(2)}, u32[]{:S(2)}) collective-permute-start(s16[352,512]{1,0:T(8,128)(2,1)S(1)} %get-tuple-element.28), channel_id=1, source_target_pairs={{0,2},{2,0},{1,3},{3,1},{4,6},{6,4},{5,7},{7,5},{8,10},{10,8},{9,1... | collective-permute-start | bytes 1081352 | tf_op jit(solution)/shard_map/ppermute | solution.py:349

commit v2 on v1

--- a/solution.py
+++ b/solution.py
@@ -15,6 +15,7 @@
 DEAL = 21
 GROUP = HALVES * SETS * DEAL
 DEAL_PAD = 24
+COPIES = 8
 STEPS = 256
 TOP = 32767.0
 
@@ -92,9 +93,23 @@
     return jnp.concatenate(wide, axis=1)
 
 
-def deal_kernel(here, code, tokens, chunk, rank, own, at):
+def deal_kernel(ids, tokens, chunk, code, rank, own, at, held, arrived):
     blocks = code.shape[0]
     per = blocks // ROWS
+    share = tokens.shape[0] // COPIES
+    copies = [
+        pltpu.make_async_copy(
+            tokens.at[pl.ds(i * share, share)], held.at[pl.ds(i * share, share)], arrived.at[i]
+        )
+        for i in range(COPIES)
+    ]
+    for copy in copies:
+        copy.start()
+    named = [((ids[0:1] == e) | (ids[1:2] == e)).astype(jnp.int32) * (1 + e) for e in range(2)]
+    named = named[0] + named[1]
+    code[...] = jnp.concatenate(
+        [named[:, i * LANES : (i + 1) * LANES] for i in range(blocks)], axis=0
+    )
     kinds = [(code[...] == k).astype(jnp.float32) for k in (1, 3, 2)]
     before = (iota((LANES, LANES), 0) < iota((LANES, LANES), 1)).astype(jnp.float32)
     ones = jnp.ones((LANES, LANES), jnp.float32)
@@ -109,14 +124,16 @@
     which = jnp.where(code[...] == 3, ranks[1], jnp.where(code[...] == 2, ranks[2], ranks[0]))
     mod = jnp.where(code[...] > 0, which & (SETS - 1), -1)
     place = sum(below(n, mod) - below(f, mod) for n, f in zip(ranks, firsts))
-    place = jnp.where(mod == here[1], place, -1)
+    place = jnp.where(mod == lax.axis_index("y"), place, -1)
     own[...] = mod
     for k in range(3):
         rank[k] = ranks[k]
     for q in range(ROWS):
         at[q, :per] = place[q * per : (q + 1) * per]
-    send = one_hot(at[here[0]][:per], SEND)
-    chunk[...] = jnp.dot(send, tokens[...], preferred_element_type=jnp.float32).astype(jnp.bfloat16)
+    send = one_hot(at[lax.axis_index("z")][:per], SEND)
+    for copy in copies:
+        copy.wait()
+    chunk[...] = jnp.dot(send, held[...], preferred_element_type=jnp.float32).astype(jnp.bfloat16)
 
 
 def lists_kernel(here, code, rank, own, at, lists, places):
@@ -200,66 +217,73 @@
     return code[:rows, span].astype(jnp.int32).astype(jnp.float32) * scale
 
 
-def product_kernel(x, *refs):
+def piece_sums(xs, span, near, far):
+    x = jnp.concatenate([x[span] for x in xs], axis=1)
+    w = jnp.concatenate([jnp.concatenate([w[0], w[1]], axis=1) for w in (near, far)], axis=0)
+    return jnp.dot(x, w, preferred_element_type=jnp.float32)
+
+
+def give_kernel(xa, xb, *refs):
     count = (len(refs) - 2) // 2
-    near, far, keep, give = refs[:count], refs[count : 2 * count], refs[-2], refs[-1]
-    n_half = keep.shape[0]
-    for j, (a, b) in enumerate(zip(near, far)):
-        w = jnp.concatenate(
-            [jnp.concatenate([a[0], a[1]], axis=1), jnp.concatenate([b[0], b[1]], axis=1)], axis=0
-        )
-        sums = jnp.dot(x[n_half:], w, preferred_element_type=jnp.float32)
-        for i in range(2):
-            coded(sums[:, i * LANES : (i + 1) * LANES], give, 2 * j + i)
-        sums = jnp.dot(x[:n_half], w, preferred_element_type=jnp.float32)
-        keep[:, 2 * j * LANES : 2 * (j + 1) * LANES] = sums
-
-
-def product(x, near, far):
-    rows, depth = x.shape
-    width = len(near) * 2 * near[0].shape[2]
+    for j in range(count):
+        sums = piece_sums((xa, xb), slice(2 * GROUP, 4 * GROUP), refs[j], refs[count + j])
+        for k in range(2):
+            for i in range(2):
+                some = sums[k * GROUP : (k + 1) * GROUP, i * LANES : (i + 1) * LANES]
+                coded(some, refs[2 * count + k], 2 * j + i)
+
+
+def keep_kernel(xa, xb, *refs):
+    count = (len(refs) - 2) // 2
+    for j in range(count):
+        sums = piece_sums((xa, xb), slice(0, 2 * GROUP), refs[j], refs[count + j])
+        for k in range(2):
+            refs[2 * count + k][:, 2 * j * LANES : 2 * (j + 1) * LANES] = sums[
+                k * GROUP : (k + 1) * GROUP
+            ]
+
+
+def product(kernel, xs, near, far, rows, kind):
+    depth = 2 * xs[0].shape[1]
+    width = len(near) * 2 * LANES
     return pl.pallas_call(
-        product_kernel,
-        out_shape=(
-            jax.ShapeDtypeStruct((rows // 2, width), jnp.float32),
-            jax.ShapeDtypeStruct((rows // 2 + 16, width), jnp.int16),
-        ),
-        in_specs=[VMEM] * (1 + 2 * len(near)),
+        kernel,
+        out_shape=(jax.ShapeDtypeStruct((rows, width), kind),) * 2,
+        in_specs=[VMEM] * (2 + 2 * len(near)),
         out_specs=(VMEM,) * 2,
         compiler_params=pltpu.CompilerParams(vmem_limit_bytes=24 << 20),
         cost_estimate=pl.CostEstimate(
-            flops=2 * rows * depth * width,
-            bytes_accessed=4 * rows * width + 2 * depth * (rows + width),
+            flops=4 * GROUP * depth * width,
+            bytes_accessed=8 * GROUP * width + 2 * depth * (2 * GROUP + width),
             transcendentals=0,
         ),
-    )(x, *near, *far)
+    )(*xs, *near, *far)
 
 
 def gated_kernel(here, *refs):
-    keeps, codes, out = refs[:2], refs[2:4], refs[4]
+    keeps, codes, out = refs[:2], refs[2:6], refs[6]
     rows = keeps[0].shape[0]
     y, core = here[1], here[4]
     for o, ahead in enumerate((0, SETS - 1, 1, 2)):
-        keep, code, j = keeps[o // 2], codes[o // 2], o % 2
-        gate, up = (
-            keep[:, (2 * j + i) * LANES : (2 * j + i + 1) * LANES] + decoded(code, 2 * j + i, rows)
-            for i in range(2)
-        )
-        hidden = gate / (1.0 + jnp.exp(-gate)) * up
         piece = (y + ahead) & (SETS - 1)
         pad = jnp.zeros((DEAL_PAD - DEAL, LANES), jnp.float32)
         for k in range(2):
+            gate, up = (
+                keeps[k][:, (2 * o + i) * LANES : (2 * o + i + 1) * LANES]
+                + decoded(codes[2 * (o // 2) + k], 2 * (o % 2) + i, rows)
+                for i in range(2)
+            )
+            hidden = gate / (1.0 + jnp.exp(-gate)) * up
             for c in range(HALVES * SETS):
-                first = k * GROUP + c * DEAL
-                some = jnp.concatenate([hidden[first : first + DEAL], pad], axis=0)
-                out[2 * c + (k ^ core), piece] = some.astype(jnp.bfloat16)
+                some = jnp.concatenate([hidden[c * DEAL : (c + 1) * DEAL], pad], axis=0)
+                out[c, k ^ core, piece] = some.astype(jnp.bfloat16)
 
 
 def placed_kernel(got, places, out):
     for e in range(2):
         for h in range(HALVES):
             lines = [
-                jnp.concatenate([got[(h * SETS + s) * 2 + e, p] for p in range(SETS)], axis=1)
+                jnp.concatenate([got[h * SETS + s, e, p] for p in range(SETS)], axis=1)
                 for s in range(SETS)
             ]
             rows = jnp.concatenate(lines, axis=0)
@@ -278,24 +302,26 @@
     near, far = weights_of_ring(w_gate, w_up, core)
 
     blocks = expert_ids.shape[0] // LANES
-    ids = expert_ids.T
-    code = sum(jnp.any(ids == e, axis=0).astype(jnp.int32) * (1 + e) for e in range(2))
-    code = code.reshape(blocks, LANES)
     low = ((x_lo * SETS + y) * QUARTERS + 2 * x_hi + core) * SLOTS_DEV
     here = jnp.stack([z, y, low, 2 * x_hi + core, core]).astype(jnp.int32)
-    chunk, rank, own, at = pl.pallas_call(
+    chunk, code, rank, own, at = pl.pallas_call(
         deal_kernel,
         out_shape=(
             jax.ShapeDtypeStruct((SEND, tokens.shape[1]), jnp.bfloat16),
+            jax.ShapeDtypeStruct((blocks, LANES), jnp.int32),
             jax.ShapeDtypeStruct((3, blocks, LANES), jnp.int32),
             jax.ShapeDtypeStruct((blocks, LANES), jnp.int32),
             jax.ShapeDtypeStruct((ROWS, 8, LANES), jnp.int32),
         ),
-        in_specs=[SMEM, VMEM, VMEM],
-        out_specs=(VMEM,) * 4,
-        compiler_params=pltpu.CompilerParams(vmem_limit_bytes=8 << 20),
+        in_specs=[VMEM, pl.BlockSpec(memory_space=pl.ANY)],
+        out_specs=(VMEM,) * 5,
+        scratch_shapes=[
+            pltpu.VMEM(tokens.shape, jnp.bfloat16),
+            pltpu.SemaphoreType.DMA((COPIES,)),
+        ],
+        compiler_params=pltpu.CompilerParams(vmem_limit_bytes=60 << 20),
         cost_estimate=pl.CostEstimate(flops=1 << 30, bytes_accessed=1 << 22, transcendentals=0),
-    )(here, code, tokens)
+    )(expert_ids.T, tokens)
     chunks = rows_of_ring(chunk)
 
     moved, places = pl.pallas_call(
@@ -333,29 +359,28 @@
     early_b = lax.ppermute(soon[n_rows:], "core", SWAP)
     late_b = lax.ppermute(chunks[-1], "core", SWAP)
     late = pick[:, 7 * SEND :]
-    x = jnp.concatenate(
-        [
-            early + jnp.dot(late, rest, preferred_element_type=jnp.float32).astype(jnp.bfloat16)
-            for early, rest in ((soon[:n_rows], chunks[-1]), (early_b, late_b))
-        ],
-        axis=1,
-    )
-
-    keeps, gots = [], []
+    xs = [
+        early + jnp.dot(late, rest, preferred_element_type=jnp.float32).astype(jnp.bfloat16)
+        for early, rest in ((soon[:n_rows], chunks[-1]), (early_b, late_b))
+    ]
+
+    gots = []
     for part in range(2):
         some = slice(2 * part, 2 * part + 2)
-        keep, give = product(x, near[some], far[some])
-        keeps.append(keep)
-        gots.append(lax.ppermute(give, "x_hi", SWAP))
+        same, cross = product(give_kernel, xs, near[some], far[some], GROUP + 8, jnp.int16)
+        gots.append(lax.ppermute(same, "x_hi", SWAP))
+        gots.append(lax.ppermute(cross, ("x_hi", "core"), [(i, 3 - i) for i in range(4)]))
+    same, cross = product(keep_kernel, xs, near, far, GROUP, jnp.float32)
+    cross = lax.ppermute(cross, "core", SWAP)
     hidden = pl.pallas_call(
         gated_kernel,
-        out_shape=jax.ShapeDtypeStruct((2 * HALVES * SETS, SETS, DEAL_PAD, LANES), jnp.bfloat16),
-        in_specs=[SMEM] + [VMEM] * 4,
+        out_shape=jax.ShapeDtypeStruct((HALVES * SETS, 2, SETS, DEAL_PAD, LANES), jnp.bfloat16),
+        in_specs=[SMEM] + [VMEM] * 6,
         out_specs=VMEM,
         compiler_params=pltpu.CompilerParams(vmem_limit_bytes=16 << 20),
         cost_estimate=pl.CostEstimate(flops=1 << 30, bytes_accessed=1 << 22, transcendentals=0),
-    )(here, *keeps, *gots)
-    hidden = lax.all_to_all(hidden, ("x_lo", "y", "core"), 0, 0)
+    )(here, same, cross, *gots)
+    hidden = lax.all_to_all(hidden, ("x_lo", "y"), 0, 0)
     return pl.pallas_call(
         placed_kernel,
         out_shape=jax.ShapeDtypeStruct((2, SLOTS_DEV, HALVES * SETS * LANES), jnp.bfloat16),

time: 159 us -> 160 us (level)
  starting transfers between devices: 32.9 us -> 37.8 us
  blocking collectives: 14.2 us -> 11.5 us
  waiting for transfers between devices: 76.6 us -> 74.2 us
  Pallas kernels: 11.9 us -> 14.2 us
  matrix products: 12.3 us -> 10.5 us
  local copies, waits for them, and re-layouts: 7.66 us -> 9.4 us
    ppermute x1, waiting for transfers between devices: 20.6 us -> 15.7 us  [weights_of_ring(): near3 = lax.ppermute(near1, 'y', y_perm(1))]
    ppermute x2 -> x5, starting transfers between devices: 3.14 us -> 7.86 us  [the longest x2 5.67 us: shards(): gots.append(lax.ppermute(same, 'x_hi', SWAP))]
    ppermute x1, waiting for transfers between devices: 0.01 us -> 4.6 us  [weights_of_ring(): far1 = lax.ppermute(far, ('y', 'core'), y_cross_perm(1))]
    all_to_all x1, blocking collectives: 14.2 us -> 11.5 us  [shards(): hidden = lax.all_to_all(hidden, ('x_lo', 'y'), 0, 0)]
    ppermute x3, waiting for transfers between devices: 20.6 us -> 18 us  [rows_of_ring(): up = lax.ppermute(up, 'z', z_perm(1))]
    pallas_call x1, Pallas kernels: 1.72 us -> 3.85 us  [shards(): pl.pallas_call(deal_kernel, out_shape=(jax.ShapeDtypeStruct((SEND, tokens...]
    ppermute x1, waiting for transfers between devices: 5.6 us -> 7.55 us  [weights_of_ring(): near1 = lax.ppermute(near, 'y', y_perm(1))]
    dot_general x2, matrix products: 3.26 us -> 1.57 us  [shards(): jnp.dot(late, rest, preferred_element_type=jnp.float32).astype(jnp.bfloat16)]
  transfers between devices with their start and end apart: 19 -> 22, of which waited for: 11 -> 13; matrix products, arithmetic and copies ran while one was open for 9% -> 8% of each run, Pallas kernels for 5% -> 4%
where the time goes in v2:
time: 160 us; the launch traced here: 159 us
  waiting for transfers between devices  74.2 us (46%)
  starting transfers between devices  37.8 us (24%)
  Pallas kernels  14.2 us (9%)
  blocking collectives  11.5 us (7%)
  matrix products  10.5 us (7%)
  local copies, waits for them, and re-layouts  9.4 us (6%)
    ppermute x3, waiting for transfers between devices, rows_of_ring(): up = lax.ppermute(up, 'z', z_perm(1))  18 us
    ppermute x1, waiting for transfers between devices, weights_of_ring(): near3 = lax.ppermute(near1, 'y', y_perm(1))  15.7 us
    all_to_all x1, blocking collectives, shards(): hidden = lax.all_to_all(hidden, ('x_lo', 'y'), 0, 0)  11.5 us
    ppermute x1, waiting for transfers between devices, weights_of_ring(): near2 = lax.ppermute(near, 'y', y_perm(-1))  10.9 us
    ppermute x3, starting transfers between devices, rows_of_ring(): down = lax.ppermute(down, 'z', z_perm(-1))  9.37 us
    ppermute x2, waiting for transfers between devices, shards(): lax.ppermute(cross, ('x_hi', 'core'), [(i, 3 - i) for i in range(4)])  8 us
    ppermute x1, waiting for transfers between devices, weights_of_ring(): near1 = lax.ppermute(near, 'y', y_perm(1))  7.55 us
    dot_general x1, matrix products, shards(): jnp.dot(both[:, :5 * SEND], jnp.concatenate(chunks[:5]), preferred_elemen...  6.62 us
  transfers between devices with their start and end apart: 22, of which 13 were waited for; matrix products, arithmetic and copies ran while one was open for 8% of the time, Pallas kernels for 4%

profile of v2, /device:TPU:1, one launch (start us, length us, event | category | flops | bytes accessed | tf_op | source)
XLA Modules:
  0.0 159.2 jit_solution(8227184210227822836)
XLA Ops:
  0.0 3.9 %shard_map.46 = (bf16[168,1536]{1,0:T(8,128)(2,1)}, s32[40,128]{1,0:T(8,128)}, s32[3,40,128]{2,1,0:T(8,128)}, s32[40,128]{1,0:T(8,128)}, s32[8,8,128]{2,1,0:T(8,128)}) custom-call(s32[2,5120]{1,0:T(2,128)} %bitcast.9, bf16[640,1536]{1,0:T(8,128)(2,1)} %tokens.1), custom_call_target="tpu_custom_call" | custom-call | flops 1073741824 | bytes 4194304 | tf_op jit(solution)/shard_map/pallas_call | solution.py:307
  3.9 2.5 %collective-permute-start = (bf16[168,1536]{1,0:T(8,128)(2,1)}, bf16[168,1536]{1,0:T(8,128)(2,1)S(1)}, u32[]{:S(2)}, u32[]{:S(2)}) collective-permute-start(bf16[168,1536]{1,0:T(8,128)(2,1)} %get-tuple-element.26), channel_id=1, source_target_pairs={{0,32},{32,64},{64,96},{96,128},{128,160},{160,192},{192,224},{224... | collective-permute-start | bytes 1548296 | tf_op jit(solution)/shard_map/ppermute | solution.py:62
  6.4 4.0 %collective-permute-start.1 = (bf16[168,1536]{1,0:T(8,128)(2,1)}, bf16[168,1536]{1,0:T(8,128)(2,1)S(1)}, u32[]{:S(2)}, u32[]{:S(2)}) collective-permute-start(bf16[168,1536]{1,0:T(8,128)(2,1)} %get-tuple-element.26), channel_id=1, source_target_pairs={{0,224},{32,0},{64,32},{96,64},{128,96},{160,128},{192,160},{224,1... | collective-permute-start | bytes 1548296 | tf_op jit(solution)/shard_map/ppermute | solution.py:63
  13.6 2.5 %shard_map.47 = (f32[8,8,168]{2,1,0:T(8,128)S(1)}, bf16[2,80,96]{2,1,0:T(8,128)(2,1)S(1)}) custom-call(s32[5]{0:T(128)S(1)} %stack.33.here, s32[40,128]{1,0:T(8,128)S(1)} %copy-done.2, s32[3,40,128]{2,1,0:T(8,128)S(1)} %copy-done, s32[40,128]{1,0:T(8,128)S(1)} %copy-done.3, s32[8,8,128]{2,1,0:T(8,128)S(1)} %copy-done.1), custom_call_target="tpu_custom_call" | custom-call | flops 1073741824 | bytes 1048576 | tf_op jit(solution)/shard_map/pallas_call | solution.py:327
  17.4 4.6 %collective-permute-done = bf16[168,1536]{1,0:T(8,128)(2,1)S(1)} collective-permute-done((bf16[168,1536]{1,0:T(8,128)(2,1)}, bf16[168,1536]{1,0:T(8,128)(2,1)S(1)}, u32[]{:S(2)}, u32[]{:S(2)}) %collective-permute-start) | collective-permute-done | bytes 516128 | tf_op jit(solution)/shard_map/ppermute | solution.py:62
  22.0 2.7 %collective-permute-start.3 = (bf16[168,1536]{1,0:T(8,128)(2,1)S(1)}, bf16[168,1536]{1,0:T(8,128)(2,1)S(1)}, u32[]{:S(2)}, u32[]{:S(2)}) collective-permute-start(bf16[168,1536]{1,0:T(8,128)(2,1)S(1)} %collective-permute-done.1), channel_id=1, source_target_pairs={{0,224},{32,0},{64,32},{96,64},{128,96},{160,128},{192,160},{224,1... | collective-permute-start | bytes 1548296 | tf_op jit(solution)/shard_map/ppermute | solution.py:63
  24.8 10.5 %collective-permute-done.2 = bf16[168,1536]{1,0:T(8,128)(2,1)S(1)} collective-permute-done((bf16[168,1536]{1,0:T(8,128)(2,1)S(1)}, bf16[168,1536]{1,0:T(8,128)(2,1)S(1)}, u32[]{:S(2)}, u32[]{:S(2)}) %collective-permute-start.2) | collective-permute-done | bytes 516128 | tf_op jit(solution)/shard_map/ppermute | solution.py:62
  35.3 2.7 %collective-permute-start.5 = (bf16[168,1536]{1,0:T(8,128)(2,1)S(1)}, bf16[168,1536]{1,0:T(8,128)(2,1)S(1)}, u32[]{:S(2)}, u32[]{:S(2)}) collective-permute-start(bf16[168,1536]{1,0:T(8,128)(2,1)S(1)} %collective-permute-done.3), channel_id=1, source_target_pairs={{0,224},{32,0},{64,32},{96,64},{128,96},{160,128},{192,160},{224,1... | collective-permute-start | bytes 1548296 | tf_op jit(solution)/shard_map/ppermute | solution.py:63
  38.0 6.6 %convolution_convert_fusion.1 = bf16[1344,1536]{1,0:T(8,128)(2,1)S(1)} fusion(bf16[840,1536]{1,0:T(8,128)(2,1)S(1)} %constant_dynamic-update-slice_fusion, pred[672,1344]{1,0:T(32,128)(4,1)S(1)} %get-tuple-element.44, pred[672,1344]{1,0:T(32,128)(4,1)S(1)} %get-tuple-element.43), kind=kOutput, calls=%fused_computation.1 | convolution fusion | flops 3471358464 | bytes 8515584 | tf_op jit(solution)/shard_map/dot_general | solution.py:349
  44.6 3.0 %collective-permute-done.4 = bf16[168,1536]{1,0:T(8,128)(2,1)S(1)} collective-permute-done((bf16[168,1536]{1,0:T(8,128)(2,1)S(1)}, bf16[168,1536]{1,0:T(8,128)(2,1)S(1)}, u32[]{:S(2)}, u32[]{:S(2)}) %collective-permute-start.4) | collective-permute-done | bytes 516128 | tf_op jit(solution)/shard_map/ppermute | solution.py:62
  47.7 2.4 %fusion.7 = bf16[1344,1536]{1,0:T(8,128)(2,1)S(1)} fusion(bf16[1344,1536]{1,0:T(8,128)(2,1)S(1)} %convolution_convert_fusion.1, pred[672,1344]{1,0:T(32,128)(4,1)S(1)} %get-tuple-element.44, pred[672,1344]{1,0:T(32,128)(4,1)S(1)} %get-tuple-element.43, bf16[168,1536]{1,0:T(8,128)(2,1)S(1)} %collective-permute-done.5, ...), kind=kOutput, calls=%fused_computation.14 | convolution fusion | flops 1393910784 | bytes 11096064 | tf_op jit(solution)/shard_map/dot_general | solution.py:353
  50.1 1.9 %copy-done.4 = bf16[1344,1536]{1,0:T(8,128)(2,1)} copy-done((bf16[1344,1536]{1,0:T(8,128)(2,1)}, bf16[1344,1536]{1,0:T(8,128)(2,1)S(1)}, u32[]{:S(2)}) %copy-start.4) | copy-done | bytes 4128792
  53.5 3.0 %collective-permute-start.8 = (bf16[672,1536]{1,0:T(8,128)(2,1)}, bf16[672,1536]{1,0:T(8,128)(2,1)S(1)}, u32[]{:S(2)}, u32[]{:S(2)}) collective-permute-start(bf16[672,1536]{1,0:T(8,128)(2,1)} %slice.52), channel_id=1, source_target_pairs={{0,1},{1,0},{2,3},{3,2},{4,5},{5,4},{6,7},{7,6},{8,9},{9,8},{10,11... | collective-permute-start | bytes 6193160 | tf_op jit(solution)/shard_map/ppermute | solution.py:359
  60.5 2.7 %collective-permute-start.7 = (bf16[80,1536]{1,0:T(8,128)(2,1)S(1)}, bf16[80,1536]{1,0:T(8,128)(2,1)S(1)}, u32[]{:S(2)}, u32[]{:S(2)}) collective-permute-start(bf16[80,1536]{1,0:T(8,128)(2,1)S(1)} %slice.51), channel_id=1, source_target_pairs={{0,224},{32,0},{64,32},{96,64},{128,96},{160,128},{192,160},{224,1... | collective-permute-start | bytes 737288 | tf_op jit(solution)/shard_map/ppermute | solution.py:67
  63.3 2.5 %collective-permute-start.15 = (bf16[2,1536,128]{2,1,0:T(8,128)(2,1)S(1)}, bf16[2,1536,128]{2,1,0:T(8,128)(2,1)S(1)}, u32[]{:S(2)}, u32[]{:S(2)}) collective-permute-start(bf16[2,1536,128]{2,1,0:T(8,128)(2,1)S(1)} %pad_maximum_fusion.1), channel_id=1, source_target_pairs={{0,13},{1,12},{4,1},{5,0},{8,5},{9,4},{12,9},{13,8},{2,15},{3,14},... | collective-permute-start | bytes 2359304 | tf_op jit(solution)/shard_map/ppermute | solution.py:50
  69.5 1.6 %collective-permute-start.11 = (bf16[2,1536,128]{2,1,0:T(8,128)(2,1)S(1)}, bf16[2,1536,128]{2,1,0:T(8,128)(2,1)S(1)}, u32[]{:S(2)}, u32[]{:S(2)}) collective-permute-start(bf16[2,1536,128]{2,1,0:T(8,128)(2,1)S(1)} %pad_maximum_fusion.refs_0_), channel_id=1, source_target_pairs={{0,12},{4,0},{8,4},{12,8},{1,13},{5,1},{9,5},{13,9},{2,14},{6,2},{... | collective-permute-start | bytes 2359304 | tf_op jit(solution)/shard_map/ppermute | solution.py:52
  71.1 7.6 %collective-permute-done.10.refs_1_ = bf16[2,1536,128]{2,1,0:T(8,128)(2,1)S(1)} collective-permute-done((bf16[2,1536,128]{2,1,0:T(8,128)(2,1)S(1)}, bf16[2,1536,128]{2,1,0:T(8,128)(2,1)S(1)}, u32[]{:S(2)}, u32[]{:S(2)}) %collective-permute-start.10) | collective-permute-done | bytes 786464 | tf_op jit(solution)/shard_map/ppermute | solution.py:49
  79.5 4.1 %collective-permute-done.15.refs_6_.refs_2_ = bf16[2,1536,128]{2,1,0:T(8,128)(2,1)S(1)} collective-permute-done((bf16[2,1536,128]{2,1,0:T(8,128)(2,1)S(1)}, bf16[2,1536,128]{2,1,0:T(8,128)(2,1)S(1)}, u32[]{:S(2)}, u32[]{:S(2)}) %collective-permute-start.15) | collective-permute-done | bytes 786464 | tf_op jit(solution)/shard_map/ppermute | solution.py:50
  83.6 1.7 %collective-permute-start.14 = (bf16[2,1536,128]{2,1,0:T(8,128)(2,1)S(1)}, bf16[2,1536,128]{2,1,0:T(8,128)(2,1)S(1)}, u32[]{:S(2)}, u32[]{:S(2)}) collective-permute-start(bf16[2,1536,128]{2,1,0:T(8,128)(2,1)S(1)} %pad_maximum_fusion.1), channel_id=1, source_target_pairs={{0,5},{1,4},{4,9},{5,8},{8,13},{9,12},{12,1},{13,0},{2,7},{3,6},{6... | collective-permute-start | bytes 2359304 | tf_op jit(solution)/shard_map/ppermute | solution.py:51
  86.3 1.7 %collective-permute-start.16 = (bf16[2,1536,128]{2,1,0:T(8,128)(2,1)S(1)}, bf16[2,1536,128]{2,1,0:T(8,128)(2,1)S(1)}, u32[]{:S(2)}, u32[]{:S(2)}) collective-permute-start(bf16[2,1536,128]{2,1,0:T(8,128)(2,1)S(1)} %collective-permute-done.15.refs_6_.refs_2_), channel_id=1, source_target_pairs={{0,12},{4,0},{8,4},{12,8},{1,13},{5,1},{9,5},{13,9},{2,14},{6,2},{... | collective-permute-start | bytes 2359304 | tf_op jit(solution)/shard_map/ppermute | solution.py:55
  89.5 10.9 %collective-permute-done.11.refs_2_.refs_0_ = bf16[2,1536,128]{2,1,0:T(8,128)(2,1)S(1)} collective-permute-done((bf16[2,1536,128]{2,1,0:T(8,128)(2,1)S(1)}, bf16[2,1536,128]{2,1,0:T(8,128)(2,1)S(1)}, u32[]{:S(2)}, u32[]{:S(2)}) %collective-permute-start.11) | collective-permute-done | bytes 786464 | tf_op jit(solution)/shard_map/ppermute | solution.py:52
  100.4 4.6 %collective-permute-done.14.refs_5_.refs_3_ = bf16[2,1536,128]{2,1,0:T(8,128)(2,1)S(1)} collective-permute-done((bf16[2,1536,128]{2,1,0:T(8,128)(2,1)S(1)}, bf16[2,1536,128]{2,1,0:T(8,128)(2,1)S(1)}, u32[]{:S(2)}, u32[]{:S(2)}) %collective-permute-start.14) | collective-permute-done | bytes 786464 | tf_op jit(solution)/shard_map/ppermute | solution.py:51
  105.0 15.7 %collective-permute-done.12.refs_3_.refs_1_ = bf16[2,1536,128]{2,1,0:T(8,128)(2,1)S(1)} collective-permute-done((bf16[2,1536,128]{2,1,0:T(8,128)(2,1)S(1)}, bf16[2,1536,128]{2,1,0:T(8,128)(2,1)S(1)}, u32[]{:S(2)}, u32[]{:S(2)}) %collective-permute-start.12) | collective-permute-done | bytes 786464 | tf_op jit(solution)/shard_map/ppermute | solution.py:54
  120.8 2.3 %shard_map.48 = (f32[168,1024]{1,0:T(8,128)S(1)}, f32[168,1024]{1,0:T(8,128)S(1)}) custom-call(bf16[672,1536]{1,0:T(8,128)(2,1)S(1)} %fusion.1.xa, bf16[672,1536]{1,0:T(8,128)(2,1)S(1)} %fusion.2.xb, bf16[2,1536,128]{2,1,0:T(8,128)(2,1)S(1)} %pad_maximum_fusion.refs_0_, bf16[2,1536,128]{2,1,0:T(8,128)(2,1)S(1)} %collective-permute-done.10.refs_1_, ...), custom_call_target="tpu_custom_call" | custom-call | flops 2113929216 | bytes 9732096 | tf_op jit(solution)/shard_map/pallas_call | solution.py:249
  124.2 1.6 shard_map.49
  125.8 2.8 %collective-permute-start.18 = (s16[176,512]{1,0:T(8,128)(2,1)S(1)}, s16[176,512]{1,0:T(8,128)(2,1)S(1)}, u32[]{:S(2)}, u32[]{:S(2)}) collective-permute-start(s16[176,512]{1,0:T(8,128)(2,1)S(1)} %get-tuple-element.32), channel_id=1, source_target_pairs={{0,2},{2,0},{1,3},{3,1},{4,6},{6,4},{5,7},{7,5},{8,10},{10,8},{9,1... | collective-permute-start | bytes 540680 | tf_op jit(solution)/shard_map/ppermute | solution.py:371
  129.1 1.6 shard_map.50
  130.6 2.8 %collective-permute-start.20 = (s16[176,512]{1,0:T(8,128)(2,1)S(1)}, s16[176,512]{1,0:T(8,128)(2,1)S(1)}, u32[]{:S(2)}, u32[]{:S(2)}) collective-permute-start(s16[176,512]{1,0:T(8,128)(2,1)S(1)} %get-tuple-element.34), channel_id=1, source_target_pairs={{0,2},{2,0},{1,3},{3,1},{4,6},{6,4},{5,7},{7,5},{8,10},{10,8},{9,1... | collective-permute-start | bytes 540680 | tf_op jit(solution)/shard_map/ppermute | solution.py:371
  134.1 4.0 %collective-permute-done.19.refs_3_ = s16[176,512]{1,0:T(8,128)(2,1)S(1)} collective-permute-done((s16[176,512]{1,0:T(8,128)(2,1)S(1)}, s16[176,512]{1,0:T(8,128)(2,1)S(1)}, u32[]{:S(2)}, u32[]{:S(2)}) %collective-permute-start.19) | collective-permute-done | bytes 180256 | tf_op jit(solution)/shard_map/ppermute | solution.py:372
  138.0 3.2 %collective-permute-done.20.refs_4_ = s16[176,512]{1,0:T(8,128)(2,1)S(1)} collective-permute-done((s16[176,512]{1,0:T(8,128)(2,1)S(1)}, s16[176,512]{1,0:T(8,128)(2,1)S(1)}, u32[]{:S(2)}, u32[]{:S(2)}) %collective-permute-start.20) | collective-permute-done | bytes 180256 | tf_op jit(solution)/shard_map/ppermute | solution.py:371
  141.2 4.0 %collective-permute-done.21.refs_5_ = s16[176,512]{1,0:T(8,128)(2,1)S(1)} collective-permute-done((s16[176,512]{1,0:T(8,128)(2,1)S(1)}, s16[176,512]{1,0:T(8,128)(2,1)S(1)}, u32[]{:S(2)}, u32[]{:S(2)}) %collective-permute-start.21) | collective-permute-done | bytes 180256 | tf_op jit(solution)/shard_map/ppermute | solution.py:372
  146.7 11.5 %all_to_all.5.got = bf16[8,2,4,24,128]{4,3,2,1,0:T(8,128)(2,1)S(1)} all-to-all(bf16[8,2,4,24,128]{4,3,2,1,0:T(8,128)(2,1)S(1)} %shard_map.51), channel_id=1, replica_groups=mesh['z'=8,'x_lo'=2,'y'=4,'x_hi'=2,'core'=2] {'x_lo','y'}, dimensions={0} | all-to-all | bytes 786432 | tf_op jit(solution)/shard_map/all_to_all | solution.py:383
  (64 shorter events, 21.9 us)
Async XLA Ops:
  3.9 18.1 %collective-permute-start = (bf16[168,1536]{1,0:T(8,128)(2,1)}, bf16[168,1536]{1,0:T(8,128)(2,1)S(1)}, u32[]{:S(2)}, u32[]{:S(2)}) collective-permute-start(bf16[168,1536]{1,0:T(8,128)(2,1)} %get-tuple-element.26), channel_id=1, source_target_pairs={{0,32},{32,64},{64,96},{96,128},{128,160},{160,192},{192,224},{224... | collective-permute-start | bytes 1548296 | tf_op jit(solution)/shard_map/ppermute | solution.py:62
  6.4 15.6 %collective-permute-start.1 = (bf16[168,1536]{1,0:T(8,128)(2,1)}, bf16[168,1536]{1,0:T(8,128)(2,1)S(1)}, u32[]{:S(2)}, u32[]{:S(2)}) collective-permute-start(bf16[168,1536]{1,0:T(8,128)(2,1)} %get-tuple-element.26), channel_id=1, source_target_pairs={{0,224},{32,0},{64,32},{96,64},{128,96},{160,128},{192,160},{224,1... | collective-permute-start | bytes 1548296 | tf_op jit(solution)/shard_map/ppermute | solution.py:63
  10.5 0.8 copy-start
  11.3 0.8 copy-start.1
  12.1 0.7 copy-start.2
  12.8 0.7 copy-start.3
  13.6 11.1 %copy-start.6 = (bf16[168,1536]{1,0:T(8,128)(2,1)S(1)}, bf16[168,1536]{1,0:T(8,128)(2,1)}, u32[]{:S(2)}) copy-start(bf16[168,1536]{1,0:T(8,128)(2,1)} %get-tuple-element.26) | copy-start | bytes 1548292
  22.0 13.3 %collective-permute-start.2 = (bf16[168,1536]{1,0:T(8,128)(2,1)S(1)}, bf16[168,1536]{1,0:T(8,128)(2,1)S(1)}, u32[]{:S(2)}, u32[]{:S(2)}) collective-permute-start(bf16[168,1536]{1,0:T(8,128)(2,1)S(1)} %collective-permute-done), channel_id=1, source_target_pairs={{0,32},{32,64},{64,96},{96,128},{128,160},{160,192},{192,224},{224... | collective-permute-start | bytes 1548296 | tf_op jit(solution)/shard_map/ppermute | solution.py:62
  22.0 13.3 %collective-permute-start.3 = (bf16[168,1536]{1,0:T(8,128)(2,1)S(1)}, bf16[168,1536]{1,0:T(8,128)(2,1)S(1)}, u32[]{:S(2)}, u32[]{:S(2)}) collective-permute-start(bf16[168,1536]{1,0:T(8,128)(2,1)S(1)} %collective-permute-done.1), channel_id=1, source_target_pairs={{0,224},{32,0},{64,32},{96,64},{128,96},{160,128},{192,160},{224,1... | collective-permute-start | bytes 1548296 | tf_op jit(solution)/shard_map/ppermute | solution.py:63
  35.3 12.4 %collective-permute-start.4 = (bf16[168,1536]{1,0:T(8,128)(2,1)S(1)}, bf16[168,1536]{1,0:T(8,128)(2,1)S(1)}, u32[]{:S(2)}, u32[]{:S(2)}) collective-permute-start(bf16[168,1536]{1,0:T(8,128)(2,1)S(1)} %collective-permute-done.2), channel_id=1, source_target_pairs={{0,32},{32,64},{64,96},{96,128},{128,160},{160,192},{192,224},{224... | collective-permute-start | bytes 1548296 | tf_op jit(solution)/shard_map/ppermute | solution.py:62
  35.3 12.4 %collective-permute-start.5 = (bf16[168,1536]{1,0:T(8,128)(2,1)S(1)}, bf16[168,1536]{1,0:T(8,128)(2,1)S(1)}, u32[]{:S(2)}, u32[]{:S(2)}) collective-permute-start(bf16[168,1536]{1,0:T(8,128)(2,1)S(1)} %collective-permute-done.3), channel_id=1, source_target_pairs={{0,224},{32,0},{64,32},{96,64},{128,96},{160,128},{192,160},{224,1... | collective-permute-start | bytes 1548296 | tf_op jit(solution)/shard_map/ppermute | solution.py:63
  47.7 2.4 %copy-start.7 = (bf16[168,1536]{1,0:T(8,128)(2,1)}, bf16[168,1536]{1,0:T(8,128)(2,1)S(1)}, u32[]{:S(2)}) copy-start(bf16[168,1536]{1,0:T(8,128)(2,1)S(1)} %collective-permute-done.4) | copy-start | bytes 1548292
  47.7 2.4 %copy-start.9 = (bf16[168,1536]{1,0:T(8,128)(2,1)}, bf16[168,1536]{1,0:T(8,128)(2,1)S(1)}, u32[]{:S(2)}) copy-start(bf16[168,1536]{1,0:T(8,128)(2,1)S(1)} %collective-permute-done.5) | copy-start | bytes 1548292
  50.0 1.9 %copy-start.4 = (bf16[1344,1536]{1,0:T(8,128)(2,1)}, bf16[1344,1536]{1,0:T(8,128)(2,1)S(1)}, u32[]{:S(2)}) copy-start(bf16[1344,1536]{1,0:T(8,128)(2,1)S(1)} %fusion.7) | copy-start | bytes 12386308
  53.5 32.8 %collective-permute-start.8 = (bf16[672,1536]{1,0:T(8,128)(2,1)}, bf16[672,1536]{1,0:T(8,128)(2,1)S(1)}, u32[]{:S(2)}, u32[]{:S(2)}) collective-permute-start(bf16[672,1536]{1,0:T(8,128)(2,1)} %slice.52), channel_id=1, source_target_pairs={{0,1},{1,0},{2,3},{3,2},{4,5},{5,4},{6,7},{7,6},{8,9},{9,8},{10,11... | collective-permute-start | bytes 6193160 | tf_op jit(solution)/shard_map/ppermute | solution.py:359
  56.4 1.5 copy-start.8
  58.0 30.0 %copy-start.5 = (bf16[1344,1536]{1,0:T(8,128)(2,1)S(1)}, bf16[1344,1536]{1,0:T(8,128)(2,1)}, u32[]{:S(2)}) copy-start(bf16[1344,1536]{1,0:T(8,128)(2,1)} %copy-done.4) | copy-start | bytes 12386308
  58.0 9.3 %collective-permute-start.6 = (bf16[88,1536]{1,0:T(8,128)(2,1)S(1)}, bf16[88,1536]{1,0:T(8,128)(2,1)S(1)}, u32[]{:S(2)}, u32[]{:S(2)}) collective-permute-start(bf16[88,1536]{1,0:T(8,128)(2,1)S(1)} %slice.50), channel_id=1, source_target_pairs={{0,32},{32,64},{64,96},{96,128},{128,160},{160,192},{192,224},{224... | collective-permute-start | bytes 811016 | tf_op jit(solution)/shard_map/ppermute | solution.py:66
  58.2 20.5 %collective-permute-start.10 = (bf16[2,1536,128]{2,1,0:T(8,128)(2,1)S(1)}, bf16[2,1536,128]{2,1,0:T(8,128)(2,1)S(1)}, u32[]{:S(2)}, u32[]{:S(2)}) collective-permute-start(bf16[2,1536,128]{2,1,0:T(8,128)(2,1)S(1)} %pad_maximum_fusion.refs_0_), channel_id=1, source_target_pairs={{0,4},{4,8},{8,12},{12,0},{1,5},{5,9},{9,13},{13,1},{2,6},{6,10},{... | collective-permute-start | bytes 2359304 | tf_op jit(solution)/shard_map/ppermute | solution.py:49
  60.5 7.5 %collective-permute-start.7 = (bf16[80,1536]{1,0:T(8,128)(2,1)S(1)}, bf16[80,1536]{1,0:T(8,128)(2,1)S(1)}, u32[]{:S(2)}, u32[]{:S(2)}) collective-permute-start(bf16[80,1536]{1,0:T(8,128)(2,1)S(1)} %slice.51), channel_id=1, source_target_pairs={{0,224},{32,0},{64,32},{96,64},{128,96},{160,128},{192,160},{224,1... | collective-permute-start | bytes 737288 | tf_op jit(solution)/shard_map/ppermute | solution.py:67
  63.3 20.2 %collective-permute-start.15 = (bf16[2,1536,128]{2,1,0:T(8,128)(2,1)S(1)}, bf16[2,1536,128]{2,1,0:T(8,128)(2,1)S(1)}, u32[]{:S(2)}, u32[]{:S(2)}) collective-permute-start(bf16[2,1536,128]{2,1,0:T(8,128)(2,1)S(1)} %pad_maximum_fusion.1), channel_id=1, source_target_pairs={{0,13},{1,12},{4,1},{5,0},{8,5},{9,4},{12,9},{13,8},{2,15},{3,14},... | collective-permute-start | bytes 2359304 | tf_op jit(solution)/shard_map/ppermute | solution.py:50
  68.0 17.2 %collective-permute-start.9 = (bf16[168,1536]{1,0:T(8,128)(2,1)S(1)}, bf16[168,1536]{1,0:T(8,128)(2,1)S(1)}, u32[]{:S(2)}, u32[]{:S(2)}) collective-permute-start(bf16[168,1536]{1,0:T(8,128)(2,1)S(1)} %constant_dynamic-update-slice_fusion.5), channel_id=1, source_target_pairs={{0,1},{1,0},{2,3},{3,2},{4,5},{5,4},{6,7},{7,6},{8,9},{9,8},{10,11... | collective-permute-start | bytes 1548296 | tf_op jit(solution)/shard_map/ppermute | solution.py:360
  69.5 30.9 %collective-permute-start.11 = (bf16[2,1536,128]{2,1,0:T(8,128)(2,1)S(1)}, bf16[2,1536,128]{2,1,0:T(8,128)(2,1)S(1)}, u32[]{:S(2)}, u32[]{:S(2)}) collective-permute-start(bf16[2,1536,128]{2,1,0:T(8,128)(2,1)S(1)} %pad_maximum_fusion.refs_0_), channel_id=1, source_target_pairs={{0,12},{4,0},{8,4},{12,8},{1,13},{5,1},{9,5},{13,9},{2,14},{6,2},{... | collective-permute-start | bytes 2359304 | tf_op jit(solution)/shard_map/ppermute | solution.py:52
  78.7 21.7 %collective-permute-start.13 = (bf16[2,1536,128]{2,1,0:T(8,128)(2,1)S(1)}, bf16[2,1536,128]{2,1,0:T(8,128)(2,1)S(1)}, u32[]{:S(2)}, u32[]{:S(2)}) collective-permute-start(bf16[2,1536,128]{2,1,0:T(8,128)(2,1)S(1)} %pad_maximum_fusion.1), channel_id=1, source_target_pairs={{0,1},{1,0},{2,3},{3,2},{4,5},{5,4},{6,7},{7,6},{8,9},{9,8},{10,11... | collective-permute-start | bytes 2359304 | tf_op jit(solution)/shard_map/ppermute | solution.py:53
  83.6 21.5 %collective-permute-start.14 = (bf16[2,1536,128]{2,1,0:T(8,128)(2,1)S(1)}, bf16[2,1536,128]{2,1,0:T(8,128)(2,1)S(1)}, u32[]{:S(2)}, u32[]{:S(2)}) collective-permute-start(bf16[2,1536,128]{2,1,0:T(8,128)(2,1)S(1)} %pad_maximum_fusion.1), channel_id=1, source_target_pairs={{0,5},{1,4},{4,9},{5,8},{8,13},{9,12},{12,1},{13,0},{2,7},{3,6},{6... | collective-permute-start | bytes 2359304 | tf_op jit(solution)/shard_map/ppermute | solution.py:51
  85.3 35.5 %collective-permute-start.12 = (bf16[2,1536,128]{2,1,0:T(8,128)(2,1)S(1)}, bf16[2,1536,128]{2,1,0:T(8,128)(2,1)S(1)}, u32[]{:S(2)}, u32[]{:S(2)}) collective-permute-start(bf16[2,1536,128]{2,1,0:T(8,128)(2,1)S(1)} %collective-permute-done.10.refs_1_), channel_id=1, source_target_pairs={{0,4},{4,8},{8,12},{12,0},{1,5},{5,9},{9,13},{13,1},{2,6},{6,10},{... | collective-permute-start | bytes 2359304 | tf_op jit(solution)/shard_map/ppermute | solution.py:54
  86.3 34.5 %collective-permute-start.16 = (bf16[2,1536,128]{2,1,0:T(8,128)(2,1)S(1)}, bf16[2,1536,128]{2,1,0:T(8,128)(2,1)S(1)}, u32[]{:S(2)}, u32[]{:S(2)}) collective-permute-start(bf16[2,1536,128]{2,1,0:T(8,128)(2,1)S(1)} %collective-permute-done.15.refs_6_.refs_2_), channel_id=1, source_target_pairs={{0,12},{4,0},{8,4},{12,8},{1,13},{5,1},{9,5},{13,9},{2,14},{6,2},{... | collective-permute-start | bytes 2359304 | tf_op jit(solution)/shard_map/ppermute | solution.py:55
  123.1 22.2 %collective-permute-start.17 = (f32[168,1024]{1,0:T(8,128)S(1)}, f32[168,1024]{1,0:T(8,128)S(1)}, u32[]{:S(2)}, u32[]{:S(2)}) collective-permute-start(f32[168,1024]{1,0:T(8,128)S(1)} %get-tuple-element.31), channel_id=1, source_target_pairs={{0,1},{1,0},{2,3},{3,2},{4,5},{5,4},{6,7},{7,6},{8,9},{9,8},{10,11... | collective-permute-start | bytes 2064392 | tf_op jit(solution)/shard_map/ppermute | solution.py:374
  125.8 8.2 %collective-permute-start.18 = (s16[176,512]{1,0:T(8,128)(2,1)S(1)}, s16[176,512]{1,0:T(8,128)(2,1)S(1)}, u32[]{:S(2)}, u32[]{:S(2)}) collective-permute-start(s16[176,512]{1,0:T(8,128)(2,1)S(1)} %get-tuple-element.32), channel_id=1, source_target_pairs={{0,2},{2,0},{1,3},{3,1},{4,6},{6,4},{5,7},{7,5},{8,10},{10,8},{9,1... | collective-permute-start | bytes 540680 | tf_op jit(solution)/shard_map/ppermute | solution.py:371
  128.7 9.4 %collective-permute-start.19 = (s16[176,512]{1,0:T(8,128)(2,1)S(1)}, s16[176,512]{1,0:T(8,128)(2,1)S(1)}, u32[]{:S(2)}, u32[]{:S(2)}) collective-permute-start(s16[176,512]{1,0:T(8,128)(2,1)S(1)} %get-tuple-element.33), channel_id=1, source_target_pairs={{0,3},{1,2},{2,1},{3,0},{4,7},{5,6},{6,5},{7,4},{8,11},{9,10},{10,... | collective-permute-start | bytes 540680 | tf_op jit(solution)/shard_map/ppermute | solution.py:372
  130.6 10.6 %collective-permute-start.20 = (s16[176,512]{1,0:T(8,128)(2,1)S(1)}, s16[176,512]{1,0:T(8,128)(2,1)S(1)}, u32[]{:S(2)}, u32[]{:S(2)}) collective-permute-start(s16[176,512]{1,0:T(8,128)(2,1)S(1)} %get-tuple-element.34), channel_id=1, source_target_pairs={{0,2},{2,0},{1,3},{3,1},{4,6},{6,4},{5,7},{7,5},{8,10},{10,8},{9,1... | collective-permute-start | bytes 540680 | tf_op jit(solution)/shard_map/ppermute | solution.py:371
  133.5 11.8 %collective-permute-start.21 = (s16[176,512]{1,0:T(8,128)(2,1)S(1)}, s16[176,512]{1,0:T(8,128)(2,1)S(1)}, u32[]{:S(2)}, u32[]{:S(2)}) collective-permute-start(s16[176,512]{1,0:T(8,128)(2,1)S(1)} %get-tuple-element.35), channel_id=1, source_target_pairs={{0,3},{1,2},{2,1},{3,0},{4,7},{5,6},{6,5},{7,4},{8,11},{9,10},{10,... | collective-permute-start | bytes 540680 | tf_op jit(solution)/shard_map/ppermute | solution.py:372

commit v3 on v2

--- a/solution.py
+++ b/solution.py
@@ -1,3 +1,5 @@
+import functools
+
 import jax
 import jax.numpy as jnp
 from jax import lax
@@ -15,7 +17,7 @@
 DEAL = 21
 GROUP = HALVES * SETS * DEAL
 DEAL_PAD = 24
-COPIES = 8
+COPIES = 5
 STEPS = 256
 TOP = 32767.0
 
@@ -65,7 +67,7 @@
     cut = 88
     first = lax.ppermute(up[:cut], "z", z_perm(1))
     second = lax.ppermute(down[cut:], "z", z_perm(-1))
-    return got + [jnp.concatenate([first, second])]
+    return got, [first, second]
 
 
 LANES = 128
@@ -131,9 +133,12 @@
     for q in range(ROWS):
         at[q, :per] = place[q * per : (q + 1) * per]
     send = one_hot(at[lax.axis_index("z")][:per], SEND)
-    for copy in copies:
+    total = jnp.zeros(chunk.shape, jnp.float32)
+    for i, copy in enumerate(copies):
         copy.wait()
-    chunk[...] = jnp.dot(send, held[...], preferred_element_type=jnp.float32).astype(jnp.bfloat16)
+        span = slice(i * share, (i + 1) * share)
+        total += jnp.dot(send[:, span], held[span], preferred_element_type=jnp.float32)
+    chunk[...] = total.astype(jnp.bfloat16)
 
 
 def lists_kernel(here, code, rank, own, at, lists, places):
@@ -217,60 +222,167 @@
     return code[:rows, span].astype(jnp.int32).astype(jnp.float32) * scale
 
 
-def piece_sums(xs, span, near, far):
+BLOCK = 2 * GROUP
+
+
+def laid(chunks, held):
+    row = 0
+    for chunk in chunks:
+        held[row : row + chunk.shape[0]] = chunk[...]
+        row += chunk.shape[0]
+
+
+def soon_kernel(count, pick, *refs):
+    chunks, before, outs, held = refs[:count], refs[count:-3], refs[-3:-1], refs[-1]
+    laid(chunks, held)
+    half = outs[0].shape[0]
+    for k, out in enumerate(outs):
+        for row in range(0, half, BLOCK):
+            span, of = slice(row, row + BLOCK), slice(k * half + row, k * half + row + BLOCK)
+            rows = jnp.dot(pick[of], held[...], preferred_element_type=jnp.float32)
+            if before:
+                rows += before[k][span].astype(jnp.float32)
+            out[span] = rows.astype(jnp.bfloat16)
+
+
+def soon(pick, chunks, before=()):
+    rows, depth = pick.shape
+    width = chunks[0].shape[1]
+    return pl.pallas_call(
+        functools.partial(soon_kernel, len(chunks)),
+        out_shape=(jax.ShapeDtypeStruct((rows // 2, width), jnp.bfloat16),) * 2,
+        in_specs=[VMEM] * (1 + len(chunks) + len(before)),
+        out_specs=(VMEM,) * 2,
+        scratch_shapes=[pltpu.VMEM((depth, width), jnp.bfloat16)],
+        compiler_params=pltpu.CompilerParams(vmem_limit_bytes=14 << 20),
+        cost_estimate=pl.CostEstimate(
+            flops=2 * rows * depth * width, bytes_accessed=1 << 23, transcendentals=0
+        ),
+    )(pick, *chunks, *before)
+
+
+def joined(early, pick, late, out):
+    for row in range(0, out.shape[0], BLOCK):
+        span = slice(row, row + BLOCK)
+        rows = jnp.dot(pick[span], late[...], preferred_element_type=jnp.float32)
+        out[span] = (rows + early[span].astype(jnp.float32)).astype(jnp.bfloat16)
+
+
+def piece_sums(xs, span, pieces):
     x = jnp.concatenate([x[span] for x in xs], axis=1)
-    w = jnp.concatenate([jnp.concatenate([w[0], w[1]], axis=1) for w in (near, far)], axis=0)
+    w = jnp.concatenate([jnp.concatenate([w[0], w[1]], axis=1) for w in pieces], axis=0)
     return jnp.dot(x, w, preferred_element_type=jnp.float32)
+
+
+GIVE, KEEP = slice(2 * GROUP, 4 * GROUP), slice(0, 2 * GROUP)
+
+
+def coded_pair(sums, outs, j):
+    for k in range(2):
+        for i in range(2):
+            some = sums[k * GROUP : (k + 1) * GROUP, i * LANES : (i + 1) * LANES]
+            coded(some, outs[k], 2 * j + i)
+
+
+def begin_kernel(early, pick, first, second, *refs):
+    pieces, xa, begun, late = refs[:-3], refs[-3], refs[-2], refs[-1]
+    laid((first, second), late)
+    joined(early, pick, late, xa)
+    for j, near in enumerate(pieces):
+        begun[:, 2 * j * LANES : 2 * (j + 1) * LANES] = piece_sums((xa,), GIVE, (near,))
+
+
+def begin(early, pick, last, near):
+    width = len(near) * 2 * LANES
+    late = sum(part.shape[0] for part in last)
+    return pl.pallas_call(
+        begin_kernel,
+        out_shape=(
+            jax.ShapeDtypeStruct(early.shape, jnp.bfloat16),
+            jax.ShapeDtypeStruct((2 * GROUP, width), jnp.float32),
+        ),
+        in_specs=[VMEM] * (4 + len(near)),
+        out_specs=(VMEM,) * 2,
+        scratch_shapes=[pltpu.VMEM((late, early.shape[1]), jnp.bfloat16)],
+        compiler_params=pltpu.CompilerParams(vmem_limit_bytes=12 << 20),
+        cost_estimate=pl.CostEstimate(
+            flops=4 * GROUP * early.shape[1] * width, bytes_accessed=1 << 22, transcendentals=0
+        ),
+    )(early, pick, *last, *near)
+
+
+def end_kernel(begun, early, pick, first, second, *refs):
+    pieces, xb, outs, late = refs[:-4], refs[-4], refs[-3:-1], refs[-1]
+    laid((first, second), late)
+    joined(early, pick, late, xb)
+    for j, far in enumerate(pieces):
+        sums = piece_sums((xb,), GIVE, (far,))
+        coded_pair(sums + begun[:, 2 * j * LANES : 2 * (j + 1) * LANES], outs, j)
+
+
+def end(begun, early, pick, last, far):
+    late = sum(part.shape[0] for part in last)
+    width = len(far) * 2 * LANES
+    return pl.pallas_call(
+        end_kernel,
+        out_shape=(
+            jax.ShapeDtypeStruct(early.shape, jnp.bfloat16),
+            *(jax.ShapeDtypeStruct((GROUP + 8, width), jnp.int16),) * 2,
+        ),
+        in_specs=[VMEM] * (5 + len(far)),
+        out_specs=(VMEM,) * 3,
+        scratch_shapes=[pltpu.VMEM((late, early.shape[1]), jnp.bfloat16)],
+        compiler_params=pltpu.CompilerParams(vmem_limit_bytes=12 << 20),
+        cost_estimate=pl.CostEstimate(
+            flops=4 * GROUP * early.shape[1] * width, bytes_accessed=1 << 22, transcendentals=0
+        ),
+    )(begun, early, pick, *last, *far)
 
 
 def give_kernel(xa, xb, *refs):
     count = (len(refs) - 2) // 2
     for j in range(count):
-        sums = piece_sums((xa, xb), slice(2 * GROUP, 4 * GROUP), refs[j], refs[count + j])
-        for k in range(2):
-            for i in range(2):
-                some = sums[k * GROUP : (k + 1) * GROUP, i * LANES : (i + 1) * LANES]
-                coded(some, refs[2 * count + k], 2 * j + i)
+        coded_pair(piece_sums((xa, xb), GIVE, (refs[j], refs[count + j])), refs[-2:], j)
 
 
 def keep_kernel(xa, xb, *refs):
     count = (len(refs) - 2) // 2
     for j in range(count):
-        sums = piece_sums((xa, xb), slice(0, 2 * GROUP), refs[j], refs[count + j])
+        sums = piece_sums((xa, xb), KEEP, (refs[j], refs[count + j]))
         for k in range(2):
             refs[2 * count + k][:, 2 * j * LANES : 2 * (j + 1) * LANES] = sums[
                 k * GROUP : (k + 1) * GROUP
             ]
 
 
-def product(kernel, xs, near, far, rows, kind):
-    depth = 2 * xs[0].shape[1]
-    width = len(near) * 2 * LANES
+def product(kernel, xs, pieces, width, rows, kind):
+    depth = 2 * xs[1].shape[1]
     return pl.pallas_call(
         kernel,
         out_shape=(jax.ShapeDtypeStruct((rows, width), kind),) * 2,
-        in_specs=[VMEM] * (2 + 2 * len(near)),
+        in_specs=[VMEM] * (len(xs) + len(pieces)),
         out_specs=(VMEM,) * 2,
-        compiler_params=pltpu.CompilerParams(vmem_limit_bytes=24 << 20),
+        compiler_params=pltpu.CompilerParams(vmem_limit_bytes=14 << 20),
         cost_estimate=pl.CostEstimate(
             flops=4 * GROUP * depth * width,
             bytes_accessed=8 * GROUP * width + 2 * depth * (2 * GROUP + width),
             transcendentals=0,
         ),
-    )(*xs, *near, *far)
-
-
-def gated_kernel(here, *refs):
-    keeps, codes, out = refs[:2], refs[2:6], refs[6]
+    )(*xs, *pieces)
+
+
+def gated_kernel(first, here, *refs):
+    keeps, codes, out = refs[:2], refs[2:4], refs[-1]
     rows = keeps[0].shape[0]
     y, core = here[1], here[4]
-    for o, ahead in enumerate((0, SETS - 1, 1, 2)):
-        piece = (y + ahead) & (SETS - 1)
+    for j in range(2):
+        o = first + j
+        piece = (y + (0, SETS - 1, 1, 2)[o]) & (SETS - 1)
         pad = jnp.zeros((DEAL_PAD - DEAL, LANES), jnp.float32)
         for k in range(2):
             gate, up = (
                 keeps[k][:, (2 * o + i) * LANES : (2 * o + i + 1) * LANES]
-                + decoded(codes[2 * (o // 2) + k], 2 * (o % 2) + i, rows)
+                + decoded(codes[k], 2 * j + i, rows)
                 for i in range(2)
             )
             hidden = gate / (1.0 + jnp.exp(-gate)) * up
@@ -322,7 +434,7 @@
         compiler_params=pltpu.CompilerParams(vmem_limit_bytes=60 << 20),
         cost_estimate=pl.CostEstimate(flops=1 << 30, bytes_accessed=1 << 22, transcendentals=0),
     )(expert_ids.T, tokens)
-    chunks = rows_of_ring(chunk)
+    chunks, last = rows_of_ring(chunk)
 
     moved, places = pl.pallas_call(
         lists_kernel,
@@ -345,41 +457,39 @@
     )
 
     both = jnp.concatenate([pick, other])
-    n_rows = QUARTERS * GROUP
-    soon = jnp.dot(
-        both[:, : 5 * SEND], jnp.concatenate(chunks[:5]), preferred_element_type=jnp.float32
-    ).astype(jnp.bfloat16)
-    soon, *middle = lax.optimization_barrier((soon, *chunks[5:7]))
-    soon = jnp.dot(
-        both[:, 5 * SEND : 7 * SEND],
-        jnp.concatenate(middle),
-        preferred_element_type=jnp.float32,
-    ).astype(jnp.bfloat16) + soon
-    soon = lax.optimization_barrier(soon)
-    early_b = lax.ppermute(soon[n_rows:], "core", SWAP)
-    late_b = lax.ppermute(chunks[-1], "core", SWAP)
+    own, give = soon(both[:, : 5 * SEND], chunks[:5])
+    own, give = soon(both[:, 5 * SEND : 7 * SEND], chunks[5:], (own, give))
+    early_b = lax.ppermute(give, "core", SWAP)
+    last_b = [lax.ppermute(part, "core", SWAP) for part in last]
     late = pick[:, 7 * SEND :]
-    xs = [
-        early + jnp.dot(late, rest, preferred_element_type=jnp.float32).astype(jnp.bfloat16)
-        for early, rest in ((soon[:n_rows], chunks[-1]), (early_b, late_b))
+    width = 4 * LANES
+    xa, begun = begin(own, late, last, near[:2])
+    xb, *first = end(begun, early_b, late, last_b, far[:2])
+    xs = (xa, xb)
+    gives = [
+        lambda: first,
+        lambda: product(give_kernel, xs, near[2:] + far[2:], width, GROUP + 8, jnp.int16),
     ]
-
     gots = []
-    for part in range(2):
-        some = slice(2 * part, 2 * part + 2)
-        same, cross = product(give_kernel, xs, near[some], far[some], GROUP + 8, jnp.int16)
+    for give in gives:
+        same, cross = give()
         gots.append(lax.ppermute(same, "x_hi", SWAP))
         gots.append(lax.ppermute(cross, ("x_hi", "core"), [(i, 3 - i) for i in range(4)]))
-    same, cross = product(keep_kernel, xs, near, far, GROUP, jnp.float32)
+    same, cross = product(keep_kernel, xs, near + far, 2 * width, GROUP, jnp.float32)
     cross = lax.ppermute(cross, "core", SWAP)
-    hidden = pl.pallas_call(
-        gated_kernel,
-        out_shape=jax.ShapeDtypeStruct((HALVES * SETS, 2, SETS, DEAL_PAD, LANES), jnp.bfloat16),
-        in_specs=[SMEM] + [VMEM] * 6,
-        out_specs=VMEM,
-        compiler_params=pltpu.CompilerParams(vmem_limit_bytes=16 << 20),
-        cost_estimate=pl.CostEstimate(flops=1 << 30, bytes_accessed=1 << 22, transcendentals=0),
-    )(here, same, cross, *gots)
+    hidden = ()
+    for part in range(2):
+        hidden = pl.pallas_call(
+            functools.partial(gated_kernel, 2 * part),
+            out_shape=jax.ShapeDtypeStruct((HALVES * SETS, 2, SETS, DEAL_PAD, LANES), jnp.bfloat16),
+            in_specs=[SMEM] + [VMEM] * (4 + len(hidden)),
+            out_specs=VMEM,
+            input_output_aliases={5: 0} if hidden else {},
+            compiler_params=pltpu.CompilerParams(vmem_limit_bytes=8 << 20),
+            cost_estimate=pl.CostEstimate(flops=1 << 29, bytes_accessed=1 << 21, transcendentals=0),
+        )(here, same, cross, *gots[2 * part : 2 * part + 2], *hidden)
+        hidden = (hidden,)
+    hidden = hidden[0]
     hidden = lax.all_to_all(hidden, ("x_lo", "y"), 0, 0)
     return pl.pallas_call(
         placed_kernel,

time: 160 us -> 164 us (1.025)
  waiting for transfers between devices: 74.2 us -> 86.8 us
  matrix products: 10.5 us -> 0 us
  Pallas kernels: 14.2 us -> 22.6 us
  local copies, waits for them, and re-layouts: 9.4 us -> 3.6 us
  starting transfers between devices: 37.8 us -> 35.8 us
    ppermute x1, waiting for transfers between devices: 0.01 us -> 14.4 us  [weights_of_ring(): far3 = lax.ppermute(far2, 'y', y_perm(-1))]
    ppermute x1, waiting for transfers between devices: 15.7 us -> 2.45 us  [weights_of_ring(): near3 = lax.ppermute(near1, 'y', y_perm(1))]
    dot_general x4 -> x0, matrix products: 10.5 us -> none  [the longest x1 6.62 us: shards(): jnp.dot(both[:, :5 * SEND], jnp.concatenate(chunks[:5]), preferred_elemen...]
    pallas_call x1 -> x6, Pallas kernels: 1.47 us -> 11.6 us  [the longest x2 6.75 us: soon(): pl.pallas_call(functools.partial(soon_kernel, len(chunks)), out_shape=(ja...]
    ppermute x1, waiting for transfers between devices: 4.6 us -> 14.2 us  [weights_of_ring(): far1 = lax.ppermute(far, ('y', 'core'), y_cross_perm(1))]
    ppermute x1, waiting for transfers between devices: 7.55 us -> 15.7 us  [weights_of_ring(): near1 = lax.ppermute(near, 'y', y_perm(1))]
    ppermute x1, waiting for transfers between devices: 4.08 us -> 0.01 us  [weights_of_ring(): far2 = lax.ppermute(far, ('y', 'core'), y_cross_perm(-1))]
    unnamed x25 -> x14, local copies, waits for them, and re-layouts: 5.14 us -> 3.06 us
  transfers between devices with their start and end apart: 22 -> 23, of which waited for: 13 -> 12; matrix products, arithmetic and copies ran while one was open for 8% -> 2% of each run, Pallas kernels for 4% -> 8%
where the time goes in v3:
time: 164 us
  waiting for transfers between devices  86.8 us (53%)
  starting transfers between devices  35.8 us (22%)
  Pallas kernels  22.6 us (14%)
  blocking collectives  12.7 us (8%)
  local copies, waits for them, and re-layouts  3.6 us (2%)
  other arithmetic  1.91 us (1%)
    ppermute x3, waiting for transfers between devices, rows_of_ring(): up = lax.ppermute(up, 'z', z_perm(1))  19.6 us
    ppermute x1, waiting for transfers between devices, weights_of_ring(): near1 = lax.ppermute(near, 'y', y_perm(1))  15.7 us
    ppermute x1, waiting for transfers between devices, weights_of_ring(): far3 = lax.ppermute(far2, 'y', y_perm(-1))  14.4 us
    ppermute x1, waiting for transfers between devices, weights_of_ring(): far1 = lax.ppermute(far, ('y', 'core'), y_cross_perm(1))  14.2 us
    all_to_all x1, blocking collectives, shards(): hidden = lax.all_to_all(hidden, ('x_lo', 'y'), 0, 0)  12.7 us
    ppermute x3, starting transfers between devices, rows_of_ring(): down = lax.ppermute(down, 'z', z_perm(-1))  9.38 us
    ppermute x1, waiting for transfers between devices, weights_of_ring(): near2 = lax.ppermute(near, 'y', y_perm(-1))  9.11 us
    ppermute x2, waiting for transfers between devices, shards(): lax.ppermute(cross, ('x_hi', 'core'), [(i, 3 - i) for i in range(4)])  8.17 us
  transfers between devices with their start and end apart: 23, of which 12 were waited for; matrix products, arithmetic and copies ran while one was open for 2% of the time, Pallas kernels for 8%

profile of v3, /device:TPU:1, one launch (start us, length us, event | category | flops | bytes accessed | tf_op | source)
XLA Modules:
  0.0 163.6 jit_solution(6894136231963020109)
XLA Ops:
  0.0 3.6 %shard_map.46 = (bf16[168,1536]{1,0:T(8,128)(2,1)}, s32[40,128]{1,0:T(8,128)}, s32[3,40,128]{2,1,0:T(8,128)}, s32[40,128]{1,0:T(8,128)}, s32[8,8,128]{2,1,0:T(8,128)}) custom-call(s32[2,5120]{1,0:T(2,128)} %bitcast.6, bf16[640,1536]{1,0:T(8,128)(2,1)} %tokens.1), custom_call_target="tpu_custom_call" | custom-call | flops 1073741824 | bytes 4194304 | tf_op jit(solution)/shard_map/pallas_call | solution.py:419
  3.6 2.5 %collective-permute-start = (bf16[168,1536]{1,0:T(8,128)(2,1)}, bf16[168,1536]{1,0:T(8,128)(2,1)S(1)}, u32[]{:S(2)}, u32[]{:S(2)}) collective-permute-start(bf16[168,1536]{1,0:T(8,128)(2,1)} %get-tuple-element.30.refs_0_), channel_id=1, source_target_pairs={{0,32},{32,64},{64,96},{96,128},{128,160},{160,192},{192,224},{224... | collective-permute-start | bytes 1548296 | tf_op jit(solution)/shard_map/ppermute | solution.py:64
  6.2 4.0 %collective-permute-start.3 = (bf16[168,1536]{1,0:T(8,128)(2,1)}, bf16[168,1536]{1,0:T(8,128)(2,1)S(1)}, u32[]{:S(2)}, u32[]{:S(2)}) collective-permute-start(bf16[168,1536]{1,0:T(8,128)(2,1)} %get-tuple-element.30.refs_0_), channel_id=1, source_target_pairs={{0,224},{32,0},{64,32},{96,64},{128,96},{160,128},{192,160},{224,1... | collective-permute-start | bytes 1548296 | tf_op jit(solution)/shard_map/ppermute | solution.py:65
  13.3 2.5 %shard_map.47 = (f32[8,8,168]{2,1,0:T(8,128)S(1)}, bf16[2,80,96]{2,1,0:T(8,128)(2,1)S(1)}) custom-call(s32[5]{0:T(128)S(1)} %stack.33.here, s32[40,128]{1,0:T(8,128)S(1)} %copy-done.3, s32[3,40,128]{2,1,0:T(8,128)S(1)} %copy-done.1, s32[40,128]{1,0:T(8,128)S(1)} %copy-done.4, s32[8,8,128]{2,1,0:T(8,128)S(1)} %copy-done.2), custom_call_target="tpu_custom_call" | custom-call | flops 1073741824 | bytes 1048576 | tf_op jit(solution)/shard_map/pallas_call | solution.py:439
  17.2 4.5 %collective-permute-done.refs_1_ = bf16[168,1536]{1,0:T(8,128)(2,1)S(1)} collective-permute-done((bf16[168,1536]{1,0:T(8,128)(2,1)}, bf16[168,1536]{1,0:T(8,128)(2,1)S(1)}, u32[]{:S(2)}, u32[]{:S(2)}) %collective-permute-start) | collective-permute-done | bytes 516128 | tf_op jit(solution)/shard_map/ppermute | solution.py:64
  21.8 2.7 %collective-permute-start.4 = (bf16[168,1536]{1,0:T(8,128)(2,1)S(1)}, bf16[168,1536]{1,0:T(8,128)(2,1)S(1)}, u32[]{:S(2)}, u32[]{:S(2)}) collective-permute-start(bf16[168,1536]{1,0:T(8,128)(2,1)S(1)} %collective-permute-done.3.refs_2_), channel_id=1, source_target_pairs={{0,224},{32,0},{64,32},{96,64},{128,96},{160,128},{192,160},{224,1... | collective-permute-start | bytes 1548296 | tf_op jit(solution)/shard_map/ppermute | solution.py:65
  24.8 10.3 %collective-permute-done.1.refs_3_ = bf16[168,1536]{1,0:T(8,128)(2,1)S(1)} collective-permute-done((bf16[168,1536]{1,0:T(8,128)(2,1)S(1)}, bf16[168,1536]{1,0:T(8,128)(2,1)S(1)}, u32[]{:S(2)}, u32[]{:S(2)}) %collective-permute-start.1) | collective-permute-done | bytes 516128 | tf_op jit(solution)/shard_map/ppermute | solution.py:64
  35.0 2.7 %collective-permute-start.5 = (bf16[168,1536]{1,0:T(8,128)(2,1)S(1)}, bf16[168,1536]{1,0:T(8,128)(2,1)S(1)}, u32[]{:S(2)}, u32[]{:S(2)}) collective-permute-start(bf16[168,1536]{1,0:T(8,128)(2,1)S(1)} %collective-permute-done.4.refs_4_), channel_id=1, source_target_pairs={{0,224},{32,0},{64,32},{96,64},{128,96},{160,128},{192,160},{224,1... | collective-permute-start | bytes 1548296 | tf_op jit(solution)/shard_map/ppermute | solution.py:65
  38.2 4.4 %shard_map.48 = (bf16[672,1536]{1,0:T(8,128)(2,1)S(1)}, bf16[672,1536]{1,0:T(8,128)(2,1)S(1)}) custom-call(bf16[1344,840]{1,0:T(8,128)(2,1)S(1)} %pad_maximum_fusion.pick, bf16[168,1536]{1,0:T(8,128)(2,1)S(1)} %copy-done, bf16[168,1536]{1,0:T(8,128)(2,1)S(1)} %collective-permute-done.refs_1_, bf16[168,1536]{1,0:T(8,128)(2,1)S(1)} %collective-permute-done.3.refs_2_, ...), custom_call_target="tpu_custom_call" | custom-call | flops 3468165120 | bytes 8388608 | tf_op jit(solution)/shard_map/pallas_call | solution.py:251
  42.6 4.8 %collective-permute-done.2.refs_0_ = bf16[168,1536]{1,0:T(8,128)(2,1)S(1)} collective-permute-done((bf16[168,1536]{1,0:T(8,128)(2,1)S(1)}, bf16[168,1536]{1,0:T(8,128)(2,1)S(1)}, u32[]{:S(2)}, u32[]{:S(2)}) %collective-permute-start.2) | collective-permute-done | bytes 516128 | tf_op jit(solution)/shard_map/ppermute | solution.py:64
  47.5 2.3 %shard_map.49 = (bf16[672,1536]{1,0:T(8,128)(2,1)S(1)}, bf16[672,1536]{1,0:T(8,128)(2,1)S(1)}) custom-call(bf16[1344,336]{1,0:T(8,128)(2,1)S(1)} %pad_maximum_fusion.1.pick, bf16[168,1536]{1,0:T(8,128)(2,1)S(1)} %collective-permute-done.2.refs_0_, bf16[168,1536]{1,0:T(8,128)(2,1)S(1)} %collective-permute-done.5.refs_1_, ...), custom_call_target="tpu_custom_call" | custom-call | flops 1387266048 | bytes 8388608 | tf_op jit(solution)/shard_map/pallas_call | solution.py:251
  49.8 3.1 %collective-permute-start.9 = (bf16[672,1536]{1,0:T(8,128)(2,1)S(1)}, bf16[672,1536]{1,0:T(8,128)(2,1)S(1)}, u32[]{:S(2)}, u32[]{:S(2)}) collective-permute-start(bf16[672,1536]{1,0:T(8,128)(2,1)S(1)} %get-tuple-element.36), channel_id=1, source_target_pairs={{0,1},{1,0},{2,3},{3,2},{4,5},{5,4},{6,7},{7,6},{8,9},{9,8},{10,11... | collective-permute-start | bytes 6193160 | tf_op jit(solution)/shard_map/ppermute | solution.py:462
  52.9 1.4 collective-permute-start.8
  54.7 1.4 collective-permute-start.13
  56.1 1.6 collective-permute-start.16
  57.7 15.7 %collective-permute-done.8.refs_1_ = bf16[2,1536,128]{2,1,0:T(8,128)(2,1)S(1)} collective-permute-done((bf16[2,1536,128]{2,1,0:T(8,128)(2,1)S(1)}, bf16[2,1536,128]{2,1,0:T(8,128)(2,1)S(1)}, u32[]{:S(2)}, u32[]{:S(2)}) %collective-permute-start.8) | collective-permute-done | bytes 786464 | tf_op jit(solution)/shard_map/ppermute | solution.py:51
  73.4 2.7 %collective-permute-start.7 = (bf16[80,1536]{1,0:T(8,128)(2,1)S(1)}, bf16[80,1536]{1,0:T(8,128)(2,1)S(1)}, u32[]{:S(2)}, u32[]{:S(2)}) collective-permute-start(bf16[80,1536]{1,0:T(8,128)(2,1)S(1)} %slice.42), channel_id=1, source_target_pairs={{0,224},{32,0},{64,32},{96,64},{128,96},{160,128},{192,160},{224,1... | collective-permute-start | bytes 737288 | tf_op jit(solution)/shard_map/ppermute | solution.py:69
  76.2 14.2 %collective-permute-done.13.refs_1_.refs_5_ = bf16[2,1536,128]{2,1,0:T(8,128)(2,1)S(1)} collective-permute-done((bf16[2,1536,128]{2,1,0:T(8,128)(2,1)S(1)}, bf16[2,1536,128]{2,1,0:T(8,128)(2,1)S(1)}, u32[]{:S(2)}, u32[]{:S(2)}) %collective-permute-start.13) | collective-permute-done | bytes 786464 | tf_op jit(solution)/shard_map/ppermute | solution.py:53
  90.4 1.5 collective-permute-start.14
  91.8 2.7 %collective-permute-start.17 = (bf16[2,1536,128]{2,1,0:T(8,128)(2,1)S(1)}, bf16[2,1536,128]{2,1,0:T(8,128)(2,1)S(1)}, u32[]{:S(2)}, u32[]{:S(2)}) collective-permute-start(bf16[2,1536,128]{2,1,0:T(8,128)(2,1)S(1)} %collective-permute-done.16.refs_6_.refs_2_), channel_id=1, source_target_pairs={{0,12},{4,0},{8,4},{12,8},{1,13},{5,1},{9,5},{13,9},{2,14},{6,2},{... | collective-permute-start | bytes 2359304 | tf_op jit(solution)/shard_map/ppermute | solution.py:57
  98.5 1.6 shard_map.51
  100.1 9.1 %collective-permute-done.14.refs_2_.refs_0_ = bf16[2,1536,128]{2,1,0:T(8,128)(2,1)S(1)} collective-permute-done((bf16[2,1536,128]{2,1,0:T(8,128)(2,1)S(1)}, bf16[2,1536,128]{2,1,0:T(8,128)(2,1)S(1)}, u32[]{:S(2)}, u32[]{:S(2)}) %collective-permute-start.14) | collective-permute-done | bytes 786464 | tf_op jit(solution)/shard_map/ppermute | solution.py:54
  109.2 2.5 %collective-permute-done.15.refs_3_.refs_1_ = bf16[2,1536,128]{2,1,0:T(8,128)(2,1)S(1)} collective-permute-done((bf16[2,1536,128]{2,1,0:T(8,128)(2,1)S(1)}, bf16[2,1536,128]{2,1,0:T(8,128)(2,1)S(1)}, u32[]{:S(2)}, u32[]{:S(2)}) %collective-permute-start.15) | collective-permute-done | bytes 786464 | tf_op jit(solution)/shard_map/ppermute | solution.py:56
  111.7 14.4 %collective-permute-done.17.refs_7_.refs_3_ = bf16[2,1536,128]{2,1,0:T(8,128)(2,1)S(1)} collective-permute-done((bf16[2,1536,128]{2,1,0:T(8,128)(2,1)S(1)}, bf16[2,1536,128]{2,1,0:T(8,128)(2,1)S(1)}, u32[]{:S(2)}, u32[]{:S(2)}) %collective-permute-start.17) | collective-permute-done | bytes 786464 | tf_op jit(solution)/shard_map/ppermute | solution.py:57
  126.1 2.3 %shard_map.52 = (f32[168,1024]{1,0:T(8,128)S(1)}, f32[168,1024]{1,0:T(8,128)S(1)}) custom-call(bf16[672,1536]{1,0:T(8,128)(2,1)S(1)} %get-tuple-element.34.xa, bf16[672,1536]{1,0:T(8,128)(2,1)S(1)} %get-tuple-element.37.xb, bf16[2,1536,128]{2,1,0:T(8,128)(2,1)S(1)} %pad_maximum_fusion.2.refs_0_, bf16[2,1536,128]{2,1,0:T(8,128)(2,1)S(1)} %collective-permute-done.8.refs_1_, ...), custom_call_target="tpu_custom_call" | custom-call | flops 2113929216 | bytes 9732096 | tf_op jit(solution)/shard_map/pallas_call | solution.py:360
  129.6 2.7 %collective-permute-start.21 = (s16[176,512]{1,0:T(8,128)(2,1)S(1)}, s16[176,512]{1,0:T(8,128)(2,1)S(1)}, u32[]{:S(2)}, u32[]{:S(2)}) collective-permute-start(s16[176,512]{1,0:T(8,128)(2,1)S(1)} %get-tuple-element.42), channel_id=1, source_target_pairs={{0,2},{2,0},{1,3},{3,1},{4,6},{6,4},{5,7},{7,5},{8,10},{10,8},{9,1... | collective-permute-start | bytes 540680 | tf_op jit(solution)/shard_map/ppermute | solution.py:476
  132.8 1.6 shard_map.53
  134.4 2.8 %collective-permute-start.19 = (s16[176,512]{1,0:T(8,128)(2,1)S(1)}, s16[176,512]{1,0:T(8,128)(2,1)S(1)}, u32[]{:S(2)}, u32[]{:S(2)}) collective-permute-start(s16[176,512]{1,0:T(8,128)(2,1)S(1)} %get-tuple-element.40), channel_id=1, source_target_pairs={{0,2},{2,0},{1,3},{3,1},{4,6},{6,4},{5,7},{7,5},{8,10},{10,8},{9,1... | collective-permute-start | bytes 540680 | tf_op jit(solution)/shard_map/ppermute | solution.py:476
  137.7 4.0 %collective-permute-done.22.refs_3_ = s16[176,512]{1,0:T(8,128)(2,1)S(1)} collective-permute-done((s16[176,512]{1,0:T(8,128)(2,1)S(1)}, s16[176,512]{1,0:T(8,128)(2,1)S(1)}, u32[]{:S(2)}, u32[]{:S(2)}) %collective-permute-start.22) | collective-permute-done | bytes 180256 | tf_op jit(solution)/shard_map/ppermute | solution.py:477
  142.8 2.0 %collective-permute-done.19.refs_2_ = s16[176,512]{1,0:T(8,128)(2,1)S(1)} collective-permute-done((s16[176,512]{1,0:T(8,128)(2,1)S(1)}, s16[176,512]{1,0:T(8,128)(2,1)S(1)}, u32[]{:S(2)}, u32[]{:S(2)}) %collective-permute-start.19) | collective-permute-done | bytes 180256 | tf_op jit(solution)/shard_map/ppermute | solution.py:476
  144.8 4.1 %collective-permute-done.20.refs_3_ = s16[176,512]{1,0:T(8,128)(2,1)S(1)} collective-permute-done((s16[176,512]{1,0:T(8,128)(2,1)S(1)}, s16[176,512]{1,0:T(8,128)(2,1)S(1)}, u32[]{:S(2)}, u32[]{:S(2)}) %collective-permute-start.20) | collective-permute-done | bytes 180256 | tf_op jit(solution)/shard_map/ppermute | solution.py:477
  150.0 12.7 %all_to_all.5.got = bf16[8,2,4,24,128]{4,3,2,1,0:T(8,128)(2,1)S(1)} all-to-all(bf16[8,2,4,24,128]{4,3,2,1,0:T(8,128)(2,1)S(1)} %shard_map.55), channel_id=1, replica_groups=mesh['z'=8,'x_lo'=2,'y'=4,'x_hi'=2,'core'=2] {'x_lo','y'}, dimensions={0} | all-to-all | bytes 786432 | tf_op jit(solution)/shard_map/all_to_all | solution.py:493
  (55 shorter events, 15.1 us)
Async XLA Ops:
  3.6 18.1 %collective-permute-start = (bf16[168,1536]{1,0:T(8,128)(2,1)}, bf16[168,1536]{1,0:T(8,128)(2,1)S(1)}, u32[]{:S(2)}, u32[]{:S(2)}) collective-permute-start(bf16[168,1536]{1,0:T(8,128)(2,1)} %get-tuple-element.30.refs_0_), channel_id=1, source_target_pairs={{0,32},{32,64},{64,96},{96,128},{128,160},{160,192},{192,224},{224... | collective-permute-start | bytes 1548296 | tf_op jit(solution)/shard_map/ppermute | solution.py:64
  6.2 15.6 %collective-permute-start.3 = (bf16[168,1536]{1,0:T(8,128)(2,1)}, bf16[168,1536]{1,0:T(8,128)(2,1)S(1)}, u32[]{:S(2)}, u32[]{:S(2)}) collective-permute-start(bf16[168,1536]{1,0:T(8,128)(2,1)} %get-tuple-element.30.refs_0_), channel_id=1, source_target_pairs={{0,224},{32,0},{64,32},{96,64},{128,96},{160,128},{192,160},{224,1... | collective-permute-start | bytes 1548296 | tf_op jit(solution)/shard_map/ppermute | solution.py:65
  10.3 0.8 copy-start.1
  11.1 0.8 copy-start.2
  11.9 0.7 copy-start.3
  12.6 0.7 copy-start.4
  15.9 8.6 %copy-start.5 = (bf16[2,1536,128]{2,1,0:T(8,128)(2,1)S(1)}, bf16[2,1536,128]{2,1,0:T(8,128)(2,1)}, u32[]{:S(2)}) copy-start(bf16[2,1536,128]{2,1,0:T(8,128)(2,1)} %param.7) | copy-start | bytes 2359300
  15.9 8.6 %copy-start.6 = (bf16[2,1536,128]{2,1,0:T(8,128)(2,1)S(1)}, bf16[2,1536,128]{2,1,0:T(8,128)(2,1)}, u32[]{:S(2)}) copy-start(bf16[2,1536,128]{2,1,0:T(8,128)(2,1)} %param.6) | copy-start | bytes 2359300
  21.8 13.3 %collective-permute-start.1 = (bf16[168,1536]{1,0:T(8,128)(2,1)S(1)}, bf16[168,1536]{1,0:T(8,128)(2,1)S(1)}, u32[]{:S(2)}, u32[]{:S(2)}) collective-permute-start(bf16[168,1536]{1,0:T(8,128)(2,1)S(1)} %collective-permute-done.refs_1_), channel_id=1, source_target_pairs={{0,32},{32,64},{64,96},{96,128},{128,160},{160,192},{192,224},{224... | collective-permute-start | bytes 1548296 | tf_op jit(solution)/shard_map/ppermute | solution.py:64
  21.8 13.3 %collective-permute-start.4 = (bf16[168,1536]{1,0:T(8,128)(2,1)S(1)}, bf16[168,1536]{1,0:T(8,128)(2,1)S(1)}, u32[]{:S(2)}, u32[]{:S(2)}) collective-permute-start(bf16[168,1536]{1,0:T(8,128)(2,1)S(1)} %collective-permute-done.3.refs_2_), channel_id=1, source_target_pairs={{0,224},{32,0},{64,32},{96,64},{128,96},{160,128},{192,160},{224,1... | collective-permute-start | bytes 1548296 | tf_op jit(solution)/shard_map/ppermute | solution.py:65
  24.8 13.4 %copy-start = (bf16[168,1536]{1,0:T(8,128)(2,1)S(1)}, bf16[168,1536]{1,0:T(8,128)(2,1)}, u32[]{:S(2)}) copy-start(bf16[168,1536]{1,0:T(8,128)(2,1)} %get-tuple-element.30.refs_0_) | copy-start | bytes 1548292
  35.0 12.4 %collective-permute-start.2 = (bf16[168,1536]{1,0:T(8,128)(2,1)S(1)}, bf16[168,1536]{1,0:T(8,128)(2,1)S(1)}, u32[]{:S(2)}, u32[]{:S(2)}) collective-permute-start(bf16[168,1536]{1,0:T(8,128)(2,1)S(1)} %collective-permute-done.1.refs_3_), channel_id=1, source_target_pairs={{0,32},{32,64},{64,96},{96,128},{128,160},{160,192},{192,224},{224... | collective-permute-start | bytes 1548296 | tf_op jit(solution)/shard_map/ppermute | solution.py:64
  35.0 12.4 %collective-permute-start.5 = (bf16[168,1536]{1,0:T(8,128)(2,1)S(1)}, bf16[168,1536]{1,0:T(8,128)(2,1)S(1)}, u32[]{:S(2)}, u32[]{:S(2)}) collective-permute-start(bf16[168,1536]{1,0:T(8,128)(2,1)S(1)} %collective-permute-done.4.refs_4_), channel_id=1, source_target_pairs={{0,224},{32,0},{64,32},{96,64},{128,96},{160,128},{192,160},{224,1... | collective-permute-start | bytes 1548296 | tf_op jit(solution)/shard_map/ppermute | solution.py:65
  49.8 48.7 %collective-permute-start.9 = (bf16[672,1536]{1,0:T(8,128)(2,1)S(1)}, bf16[672,1536]{1,0:T(8,128)(2,1)S(1)}, u32[]{:S(2)}, u32[]{:S(2)}) collective-permute-start(bf16[672,1536]{1,0:T(8,128)(2,1)S(1)} %get-tuple-element.36), channel_id=1, source_target_pairs={{0,1},{1,0},{2,3},{3,2},{4,5},{5,4},{6,7},{7,6},{8,9},{9,8},{10,11... | collective-permute-start | bytes 6193160 | tf_op jit(solution)/shard_map/ppermute | solution.py:462
  52.9 20.5 %collective-permute-start.8 = (bf16[2,1536,128]{2,1,0:T(8,128)(2,1)S(1)}, bf16[2,1536,128]{2,1,0:T(8,128)(2,1)S(1)}, u32[]{:S(2)}, u32[]{:S(2)}) collective-permute-start(bf16[2,1536,128]{2,1,0:T(8,128)(2,1)S(1)} %pad_maximum_fusion.2.refs_0_), channel_id=1, source_target_pairs={{0,4},{4,8},{8,12},{12,0},{1,5},{5,9},{9,13},{13,1},{2,6},{6,10},{... | collective-permute-start | bytes 2359304 | tf_op jit(solution)/shard_map/ppermute | solution.py:51
  54.4 21.7 %collective-permute-start.12 = (bf16[2,1536,128]{2,1,0:T(8,128)(2,1)S(1)}, bf16[2,1536,128]{2,1,0:T(8,128)(2,1)S(1)}, u32[]{:S(2)}, u32[]{:S(2)}) collective-permute-start(bf16[2,1536,128]{2,1,0:T(8,128)(2,1)S(1)} %pad_maximum_fusion.3), channel_id=1, source_target_pairs={{0,1},{1,0},{2,3},{3,2},{4,5},{5,4},{6,7},{7,6},{8,9},{9,8},{10,11... | collective-permute-start | bytes 2359304 | tf_op jit(solution)/shard_map/ppermute | solution.py:55
  54.7 35.6 %collective-permute-start.13 = (bf16[2,1536,128]{2,1,0:T(8,128)(2,1)S(1)}, bf16[2,1536,128]{2,1,0:T(8,128)(2,1)S(1)}, u32[]{:S(2)}, u32[]{:S(2)}) collective-permute-start(bf16[2,1536,128]{2,1,0:T(8,128)(2,1)S(1)} %pad_maximum_fusion.3), channel_id=1, source_target_pairs={{0,5},{1,4},{4,9},{5,8},{8,13},{9,12},{12,1},{13,0},{2,7},{3,6},{6... | collective-permute-start | bytes 2359304 | tf_op jit(solution)/shard_map/ppermute | solution.py:53
  56.1 35.7 %collective-permute-start.16 = (bf16[2,1536,128]{2,1,0:T(8,128)(2,1)S(1)}, bf16[2,1536,128]{2,1,0:T(8,128)(2,1)S(1)}, u32[]{:S(2)}, u32[]{:S(2)}) collective-permute-start(bf16[2,1536,128]{2,1,0:T(8,128)(2,1)S(1)} %pad_maximum_fusion.3), channel_id=1, source_target_pairs={{0,13},{1,12},{4,1},{5,0},{8,5},{9,4},{12,9},{13,8},{2,15},{3,14},... | collective-permute-start | bytes 2359304 | tf_op jit(solution)/shard_map/ppermute | solution.py:52
  73.4 18.5 %collective-permute-start.7 = (bf16[80,1536]{1,0:T(8,128)(2,1)S(1)}, bf16[80,1536]{1,0:T(8,128)(2,1)S(1)}, u32[]{:S(2)}, u32[]{:S(2)}) collective-permute-start(bf16[80,1536]{1,0:T(8,128)(2,1)S(1)} %slice.42), channel_id=1, source_target_pairs={{0,224},{32,0},{64,32},{96,64},{128,96},{160,128},{192,160},{224,1... | collective-permute-start | bytes 737288 | tf_op jit(solution)/shard_map/ppermute | solution.py:69
  76.1 18.4 %collective-permute-start.6 = (bf16[88,1536]{1,0:T(8,128)(2,1)S(1)}, bf16[88,1536]{1,0:T(8,128)(2,1)S(1)}, u32[]{:S(2)}, u32[]{:S(2)}) collective-permute-start(bf16[88,1536]{1,0:T(8,128)(2,1)S(1)} %slice.41), channel_id=1, source_target_pairs={{0,32},{32,64},{64,96},{96,128},{128,160},{160,192},{192,224},{224... | collective-permute-start | bytes 811016 | tf_op jit(solution)/shard_map/ppermute | solution.py:68
  90.4 18.8 %collective-permute-start.14 = (bf16[2,1536,128]{2,1,0:T(8,128)(2,1)S(1)}, bf16[2,1536,128]{2,1,0:T(8,128)(2,1)S(1)}, u32[]{:S(2)}, u32[]{:S(2)}) collective-permute-start(bf16[2,1536,128]{2,1,0:T(8,128)(2,1)S(1)} %pad_maximum_fusion.2.refs_0_), channel_id=1, source_target_pairs={{0,12},{4,0},{8,4},{12,8},{1,13},{5,1},{9,5},{13,9},{2,14},{6,2},{... | collective-permute-start | bytes 2359304 | tf_op jit(solution)/shard_map/ppermute | solution.py:54
  91.8 19.8 %collective-permute-start.15 = (bf16[2,1536,128]{2,1,0:T(8,128)(2,1)S(1)}, bf16[2,1536,128]{2,1,0:T(8,128)(2,1)S(1)}, u32[]{:S(2)}, u32[]{:S(2)}) collective-permute-start(bf16[2,1536,128]{2,1,0:T(8,128)(2,1)S(1)} %collective-permute-done.8.refs_1_), channel_id=1, source_target_pairs={{0,4},{4,8},{8,12},{12,0},{1,5},{5,9},{9,13},{13,1},{2,6},{6,10},{... | collective-permute-start | bytes 2359304 | tf_op jit(solution)/shard_map/ppermute | solution.py:56
  91.8 34.2 %collective-permute-start.17 = (bf16[2,1536,128]{2,1,0:T(8,128)(2,1)S(1)}, bf16[2,1536,128]{2,1,0:T(8,128)(2,1)S(1)}, u32[]{:S(2)}, u32[]{:S(2)}) collective-permute-start(bf16[2,1536,128]{2,1,0:T(8,128)(2,1)S(1)} %collective-permute-done.16.refs_6_.refs_2_), channel_id=1, source_target_pairs={{0,12},{4,0},{8,4},{12,8},{1,13},{5,1},{9,5},{13,9},{2,14},{6,2},{... | collective-permute-start | bytes 2359304 | tf_op jit(solution)/shard_map/ppermute | solution.py:57
  94.5 2.2 %collective-permute-start.11 = (bf16[80,1536]{1,0:T(8,128)(2,1)S(1)}, bf16[80,1536]{1,0:T(8,128)(2,1)S(1)}, u32[]{:S(2)}, u32[]{:S(2)}) collective-permute-start(bf16[80,1536]{1,0:T(8,128)(2,1)S(1)} %collective-permute-done.7.second), channel_id=1, source_target_pairs={{0,1},{1,0},{2,3},{3,2},{4,5},{5,4},{6,7},{7,6},{8,9},{9,8},{10,11... | collective-permute-start | bytes 737288 | tf_op jit(solution)/shard_map/ppermute | solution.py:463
  96.7 1.8 %collective-permute-start.10 = (bf16[88,1536]{1,0:T(8,128)(2,1)S(1)}, bf16[88,1536]{1,0:T(8,128)(2,1)S(1)}, u32[]{:S(2)}, u32[]{:S(2)}) collective-permute-start(bf16[88,1536]{1,0:T(8,128)(2,1)S(1)} %collective-permute-done.6.first), channel_id=1, source_target_pairs={{0,1},{1,0},{2,3},{3,2},{4,5},{5,4},{6,7},{7,6},{8,9},{9,8},{10,11... | collective-permute-start | bytes 811016 | tf_op jit(solution)/shard_map/ppermute | solution.py:463
  128.4 13.4 %collective-permute-start.18 = (f32[168,1024]{1,0:T(8,128)S(1)}, f32[168,1024]{1,0:T(8,128)S(1)}, u32[]{:S(2)}, u32[]{:S(2)}) collective-permute-start(f32[168,1024]{1,0:T(8,128)S(1)} %get-tuple-element.39), channel_id=1, source_target_pairs={{0,1},{1,0},{2,3},{3,2},{4,5},{5,4},{6,7},{7,6},{8,9},{9,8},{10,11... | collective-permute-start | bytes 2064392 | tf_op jit(solution)/shard_map/ppermute | solution.py:479
  129.6 8.2 %collective-permute-start.21 = (s16[176,512]{1,0:T(8,128)(2,1)S(1)}, s16[176,512]{1,0:T(8,128)(2,1)S(1)}, u32[]{:S(2)}, u32[]{:S(2)}) collective-permute-start(s16[176,512]{1,0:T(8,128)(2,1)S(1)} %get-tuple-element.42), channel_id=1, source_target_pairs={{0,2},{2,0},{1,3},{3,1},{4,6},{6,4},{5,7},{7,5},{8,10},{10,8},{9,1... | collective-permute-start | bytes 540680 | tf_op jit(solution)/shard_map/ppermute | solution.py:476
  132.3 9.5 %collective-permute-start.22 = (s16[176,512]{1,0:T(8,128)(2,1)S(1)}, s16[176,512]{1,0:T(8,128)(2,1)S(1)}, u32[]{:S(2)}, u32[]{:S(2)}) collective-permute-start(s16[176,512]{1,0:T(8,128)(2,1)S(1)} %get-tuple-element.43), channel_id=1, source_target_pairs={{0,3},{1,2},{2,1},{3,0},{4,7},{5,6},{6,5},{7,4},{8,11},{9,10},{10,... | collective-permute-start | bytes 540680 | tf_op jit(solution)/shard_map/ppermute | solution.py:477
  134.4 10.4 %collective-permute-start.19 = (s16[176,512]{1,0:T(8,128)(2,1)S(1)}, s16[176,512]{1,0:T(8,128)(2,1)S(1)}, u32[]{:S(2)}, u32[]{:S(2)}) collective-permute-start(s16[176,512]{1,0:T(8,128)(2,1)S(1)} %get-tuple-element.40), channel_id=1, source_target_pairs={{0,2},{2,0},{1,3},{3,1},{4,6},{6,4},{5,7},{7,5},{8,10},{10,8},{9,1... | collective-permute-start | bytes 540680 | tf_op jit(solution)/shard_map/ppermute | solution.py:476
  137.2 11.8 %collective-permute-start.20 = (s16[176,512]{1,0:T(8,128)(2,1)S(1)}, s16[176,512]{1,0:T(8,128)(2,1)S(1)}, u32[]{:S(2)}, u32[]{:S(2)}) collective-permute-start(s16[176,512]{1,0:T(8,128)(2,1)S(1)} %get-tuple-element.41), channel_id=1, source_target_pairs={{0,3},{1,2},{2,1},{3,0},{4,7},{5,6},{6,5},{7,4},{8,11},{9,10},{10,... | collective-permute-start | bytes 540680 | tf_op jit(solution)/shard_map/ppermute | solution.py:477
